TPU v7x, 256 devices: a whole 4x4x8 slice. The times are simulated.
256 devices in a mesh: band: 8 (over y, core), col: 32 (over z, x).
Axes of the slice: x: 4, y: 4, z: 8, core: 2. Of those that a mesh axis runs over, the one named last changes fastest.
Arguments:
- source: bfloat16 [6, 4194304], P(None, ('band', 'col')), may hold values from -6 to 6
- weights: bfloat16 [65536, 128, 128], P(('band', 'col')), may hold values from -0.5 to 0.5
- source_block: int32 [65536], P(('band', 'col')), may hold values from 0 to 127
- owner_device: int32 [65536, 1], P(('band', 'col')), may hold values from 0 to 255, as said below
- target_tile: int32 [65536], P(('band', 'col')), may hold values from 0 to 112, as said below
- cutoff: int32 [512], P(('band', 'col')), may hold values from 1 to 511
Outputs:
- remapped: float32 [6, 512, 7200], P(None, 'band', 'col')
- filtered: float32 [6, 512, 7200], P(None, 'band', 'col')
Inputs may be any that keep to these rules, and one draw needn't show every extreme that they name: `owner_device`: owners are numbered band index times 32 plus col index. A device's blocks go only to owners in its own band or in the bands next to it. Among the 256 blocks of one device at most 6 share an owner; in every device exactly 6 do for some owner of its own band, and exactly 6 for some owner of each band next to its own; every device sends at least 4 blocks to each owner of its own band. `target_tile`: every tile of every owner receives at least one block.
All inputs are finite; a program needn't handle non-finite values.
Results may differ from a plain program's by a relative error of at most 0.0003.
Values sent between devices are 32-bit elements; how exact they have to be, the bound alone decides.
A program may use at most 64 MiB of HBM per device.

v0:
```python
import jax
import jax.numpy as jnp
from jax import lax
from jax.sharding import PartitionSpec as P

NLON = 7200
KW = 512


TWO_PI = 6.283185307179586


def extended(array, sides, width):
    for axis, dim in sides:
        size, length = (lax.axis_size(axis), array.shape[dim])
        up = [(i, (i + 1) % size) for i in range(size - 1)]
        down = [(j, i) for i, j in up]
        last = lax.slice_in_dim(array, length - width, length, axis=dim)
        leading = lax.slice_in_dim(array, 0, width, axis=dim)
        before = lax.ppermute(last, axis, up)
        after = lax.ppermute(leading, axis, down)
        array = jnp.concatenate([before, array, after], axis=dim)
    return array


def cut_along(array, dim, size):
    lengths = array.shape
    tiles = array.reshape(*lengths[:dim], size, lengths[dim] // size, *lengths[dim + 1 :])
    return jnp.moveaxis(tiles, dim, 0)


def sent_and_summed(array, axis, dim):
    size = lax.axis_size(axis)
    tiles = lax.all_to_all(cut_along(array, dim, size), axis, 0, 0, tiled=True)
    return jnp.sum(tiles, axis=0)


def joined_along(tiles, dim):
    lengths = list(tiles.shape[1:])
    lengths[dim] *= tiles.shape[0]
    return jnp.moveaxis(tiles, 0, dim).reshape(lengths)


def copy_for_each(array, axis):
    size = lax.axis_size(axis)
    return lax.all_to_all(
        jnp.broadcast_to(array[None], (size, *array.shape)), axis, 0, 0, tiled=True
    )


def collect(array, axis, dim):
    return joined_along(copy_for_each(array, axis), dim)


def zonal_table(start_index, length, period, wave_count):
    positions = start_index + lax.broadcasted_iota(jnp.int32, (length, wave_count), 0)
    wave_index = lax.broadcasted_iota(jnp.int32, (length, wave_count), 1)
    phases = positions * wave_index % period
    angles = phases.astype(jnp.float32) * (TWO_PI / period)
    return jnp.concatenate([jnp.cos(angles), jnp.sin(angles)], axis=1)


def spectral_weights(cutoffs, wave_count, period):
    wave_index = lax.broadcasted_iota(jnp.int32, (cutoffs.shape[0], wave_count), 1)
    scaled = jnp.where(wave_index == 0, 1.0, 2.0) / period
    retained = jnp.where(wave_index <= cutoffs[:, None], scaled, 0.0).astype(jnp.float32)
    return jnp.concatenate([retained, retained], axis=1)


def local(source, weights, source_block, owner_device, target_tile, cutoff):
    col_count = lax.axis_size("col")
    levels = source.shape[0]
    block_count = weights.shape[0]
    block_width = weights.shape[1]
    lat_here = cutoff.shape[0]
    lat_band = lat_here * col_count
    longitudes_here = NLON // col_count
    cell_count = lat_band * longitudes_here
    tile_count = (cell_count + block_width - 1) // block_width
    regular = (tile_count + col_count - 1) // col_count
    capacity = regular + max(
        1, (block_count - col_count * regular + 2 * col_count - 1) // (2 * col_count)
    )
    slot_total = 3 * col_count * capacity
    blocks_here = source.reshape(levels, -1, block_width)
    picked = jnp.take(blocks_here, source_block, axis=1)
    partial_value = jnp.einsum("lnb,nbt->nlt", picked, weights, preferred_element_type=jnp.float32)
    tile_rows = jnp.broadcast_to(
        target_tile.astype(jnp.float32)[:, None, None], (block_count, 1, block_width)
    )
    tagged = jnp.concatenate([partial_value, tile_rows], axis=1)
    owners = owner_device[:, 0]
    owner_band = owners // col_count
    owner_col = owners % col_count
    offset = owner_band - lax.axis_index("band") + 1
    row_index = lax.broadcasted_iota(jnp.int32, (block_count, block_count), 0)
    column_index = lax.broadcasted_iota(jnp.int32, (block_count, block_count), 1)
    earlier = (owners[None, :] == owners[:, None]) & (column_index < row_index)
    rank_within = jnp.sum(earlier.astype(jnp.int32), axis=1)
    slot_index = (offset * col_count + owner_col) * capacity + rank_within
    placing = lax.broadcasted_iota(jnp.int32, (slot_total, block_count), 0) == slot_index[None, :]
    outgoing = jnp.dot(
        placing.astype(jnp.float32),
        tagged.reshape(block_count, (levels + 1) * block_width),
        precision=lax.Precision.HIGHEST,
        preferred_element_type=jnp.float32,
    )
    outgoing = outgoing.reshape(3, col_count, capacity, levels + 1, block_width)
    moved = lax.all_to_all(outgoing, "col", split_axis=1, concat_axis=1, tiled=True)
    rimmed = extended(jnp.stack([moved[0], moved[2]]), (("band", 0),), 1)
    received = jnp.stack([rimmed[0], moved[1], rimmed[3]])
    slot_rows = received.reshape(-1, levels + 1, block_width)
    slot_owned = slot_rows[:, levels, 0].astype(jnp.int32)
    slot_data = slot_rows[:, :levels, :].reshape(-1, levels * block_width)
    chooser = (
        lax.broadcasted_iota(jnp.int32, (tile_count, slot_owned.shape[0]), 0) == slot_owned[None, :]
    ).astype(jnp.float32)
    summed = jnp.dot(
        chooser, slot_data, precision=lax.Precision.HIGHEST, preferred_element_type=jnp.float32
    )
    summed = jnp.transpose(summed.reshape(tile_count, levels, block_width), (1, 0, 2)).reshape(
        levels, tile_count * block_width
    )
    remapped = summed[:, :cell_count].reshape(levels, lat_band, longitudes_here)
    retained = spectral_weights(cutoff, KW, NLON)
    local_table = zonal_table(lax.axis_index("col") * longitudes_here, longitudes_here, NLON, KW)
    partial_spectra = jnp.dot(
        remapped.reshape(levels * lat_band, longitudes_here),
        local_table,
        precision=lax.Precision.HIGHEST,
        preferred_element_type=jnp.float32,
    )
    partial_spectra = partial_spectra.reshape(levels, lat_band, 2 * KW)
    spectrum = sent_and_summed(partial_spectra, "col", 1)
    spectrum = spectrum * retained[None]
    band_spectra = collect(spectrum, "col", 1)
    filtered = jnp.dot(
        band_spectra.reshape(levels * lat_band, 2 * KW),
        local_table.T,
        precision=lax.Precision.HIGHEST,
        preferred_element_type=jnp.float32,
    )
    filtered = filtered.reshape(levels, lat_band, longitudes_here)
    return (remapped, filtered)


def solution(mesh):
    in_specs = (
        P(None, ("band", "col")),
        P(("band", "col"), None, None),
        P(("band", "col")),
        P(("band", "col"), None),
        P(("band", "col")),
        P(("band", "col")),
    )
    out_specs = (P(None, "band", "col"), P(None, "band", "col"))
    return jax.shard_map(local, mesh=mesh, in_specs=in_specs, out_specs=out_specs, check_vma=False)
```

profile of v0, /device:TPU:16, one launch (start us, length us, event | category | flops | bytes accessed | tf_op | source)
XLA Modules:
  0.0 212.5 jit_solution(10348539314015491514)
XLA Ops:
  2.1 0.9 convert_reduce_fusion
  4.5 4.7 %fusion.12 = f32[256,6,128]{2,1,0:T(8,128)S(1)} fusion(bf16[256,128,128]{2,1,0:T(8,128)(2,1)} %param.7, bf16[256,6,128]{2,1,0:T(8,128)(2,1)S(1)} %gather_fusion, pred[256]{0:T(512)(128)(4,1)S(1)} %compare_and_fusion), kind=kOutput, calls=%fused_computation.17 | convolution fusion | flops 50528256 | bytes 9568512 | tf_op jit(solution)/shard_map/lnb,nbt->nlt/dot_general | solution.py:87
  10.2 1.2 fusion.8
  11.4 1.2 copy.35
  12.6 68.8 %all_to_all.15 = f32[3,32,6,7,128]{4,3,2,0,1:T(8,128)S(1)} all-to-all(f32[3,32,6,7,128]{4,3,2,0,1:T(8,128)S(1)} %copy.35), channel_id=1, replica_groups=mesh['band'=8,'col'=32] {'col'}, dimensions={1} | all-to-all | bytes 4128768 | tf_op jit(solution)/shard_map/all_to_all | solution.py:109
  81.8 1.9 collective-permute-start
  83.8 1.1 copy.37
  84.8 3.8 %collective-permute-start.1 = (f32[1,32,6,7,128]{4,1,3,2,0:T(8,128)}, f32[1,32,6,7,128]{4,1,3,2,0:T(8,128)}, u32[]{:S(2)}, u32[]{:S(2)}) collective-permute-start(f32[1,32,6,7,128]{4,1,3,2,0:T(8,128)} %copy.37), channel_id=1, source_target_pairs={{32,0},{64,32},{96,64},{128,96},{160,128},{192,160},{224,192},{33,... | collective-permute-start | bytes 2064392 | tf_op jit(solution)/shard_map/ppermute | solution.py:21
  88.7 2.0 fusion.21
  90.7 3.4 %collective-permute-done = f32[1,32,6,7,128]{4,1,3,2,0:T(8,128)S(1)} collective-permute-done((f32[1,32,6,7,128]{4,1,3,2,0:T(8,128)S(1)}, f32[1,32,6,7,128]{4,1,3,2,0:T(8,128)S(1)}, u32[]{:S(2)}, u32[]{:S(2)}) %collective-permute-start) | collective-permute-done | bytes 688160 | tf_op jit(solution)/shard_map/ppermute | solution.py:20
  94.5 2.7 %collective-permute-done.1 = f32[1,32,6,7,128]{4,1,3,2,0:T(8,128)} collective-permute-done((f32[1,32,6,7,128]{4,1,3,2,0:T(8,128)}, f32[1,32,6,7,128]{4,1,3,2,0:T(8,128)}, u32[]{:S(2)}, u32[]{:S(2)}) %collective-permute-start.1) | collective-permute-done | bytes 688160 | tf_op jit(solution)/shard_map/ppermute | solution.py:21
  97.2 1.5 copy.39
  99.3 10.3 %fusion.24 = s32[576]{0:T(1024)S(1)} fusion(f32[576,7,128]{2,1,0:T(8,128)S(1)} %bitcast.54), kind=kLoop, calls=%fused_computation.32 | loop fusion | flops 576 | bytes 4608 | tf_op jit(solution)/shard_map/convert_element_type | solution.py:113
  109.6 1.0 fusion.2
  111.6 1.4 convolution_bitcast_fusion
  113.0 2.4 %copy.44 = f32[32,6,2,1024]{3,2,1,0:T(2,128)} copy(f32[32,6,2,1024]{3,0,2,1:T(8,128)S(1)} %convolution_bitcast_fusion) | data formatting | bytes 3145728 | tf_op jit(solution)/shard_map/transpose | solution.py:29
  115.4 4.1 %all-to-all-start.1 = ((f32[32,6,2,1024]{3,2,1,0:T(2,128)}), f32[32,6,2,1024]{3,2,1,0:T(2,128)S(1)}, u32[]{:S(2)}, u32[]{:S(2)}) async-start(f32[32,6,2,1024]{3,2,1,0:T(2,128)} %copy.44), calls=%async_computation.1 | async-start | bytes 3145728 | tf_op jit(solution)/shard_map/all_to_all | solution.py:34
  119.7 39.7 %all-to-all-done.1 = f32[32,6,2,1024]{3,2,1,0:T(2,128)S(1)} async-done(((f32[32,6,2,1024]{3,2,1,0:T(2,128)}), f32[32,6,2,1024]{3,2,1,0:T(2,128)S(1)}, u32[]{:S(2)}, u32[]{:S(2)}) %all-to-all-start.1) | async-done | bytes 1572896 | tf_op jit(solution)/shard_map/all_to_all | solution.py:34
  159.9 1.9 broadcast_in_dim.47
  161.8 5.8 %all-to-all-start.2 = ((f32[32,6,2,1024]{3,2,1,0:T(2,128)}), f32[32,6,2,1024]{3,2,1,0:T(2,128)S(1)}, u32[]{:S(2)}, u32[]{:S(2)}) async-start(f32[32,6,2,1024]{3,2,1,0:T(2,128)} %broadcast_in_dim.47), calls=%async_computation.2 | async-start | bytes 3145728 | tf_op jit(solution)/shard_map/all_to_all | solution.py:46
  167.6 1.2 reshape.134
  168.8 38.5 %all-to-all-done.2 = f32[32,6,2,1024]{3,2,1,0:T(2,128)S(1)} async-done(((f32[32,6,2,1024]{3,2,1,0:T(2,128)}), f32[32,6,2,1024]{3,2,1,0:T(2,128)S(1)}, u32[]{:S(2)}, u32[]{:S(2)}) %all-to-all-start.2) | async-done | bytes 1572896 | tf_op jit(solution)/shard_map/all_to_all | solution.py:46
  208.0 1.1 dot_general.36
  209.1 3.3 %fusion.6 = f32[6,64,225]{2,1,0:T(8,128)} fusion(f32[6,64,1024]{2,1,0:T(8,128)S(1)} %dot_general.36, f32[225,512]{1,0:T(8,128)} %copy-done.2, f32[225,512]{1,0:T(8,128)} %copy-done.1), kind=kOutput, calls=%fused_computation.10 | convolution fusion | flops 1061913600 | bytes 2840064 | tf_op jit(solution)/shard_map/dot_general | solution.py:137
  (35 shorter events, 7.4 us)
Async XLA Ops:
  0.6 3.1 %copy-start = (bf16[6,16384]{1,0:T(8,128)(2,1)S(1)}, bf16[6,16384]{1,0:T(8,128)(2,1)}, u32[]{:S(2)}) copy-start(bf16[6,16384]{1,0:T(8,128)(2,1)} %param.6) | copy-start | bytes 589828
  9.2 0.9 copy-start.3
  81.8 12.3 %collective-permute-start = (f32[1,32,6,7,128]{4,1,3,2,0:T(8,128)S(1)}, f32[1,32,6,7,128]{4,1,3,2,0:T(8,128)S(1)}, u32[]{:S(2)}, u32[]{:S(2)}) collective-permute-start(f32[1,32,6,7,128]{4,1,3,2,0:T(8,128)S(1)} %copy.36), channel_id=1, source_target_pairs={{0,32},{32,64},{64,96},{96,128},{128,160},{160,192},{192,224},{1,3... | collective-permute-start | bytes 2064392 | tf_op jit(solution)/shard_map/ppermute | solution.py:20
  84.8 12.4 %collective-permute-start.1 = (f32[1,32,6,7,128]{4,1,3,2,0:T(8,128)}, f32[1,32,6,7,128]{4,1,3,2,0:T(8,128)}, u32[]{:S(2)}, u32[]{:S(2)}) collective-permute-start(f32[1,32,6,7,128]{4,1,3,2,0:T(8,128)} %copy.37), channel_id=1, source_target_pairs={{32,0},{64,32},{96,64},{128,96},{160,128},{192,160},{224,192},{33,... | collective-permute-start | bytes 2064392 | tf_op jit(solution)/shard_map/ppermute | solution.py:21
  90.7 20.9 %copy-start.1 = (f32[225,512]{1,0:T(8,128)}, f32[225,512]{1,0:T(8,128)S(1)}, u32[]{:S(2)}) copy-start(f32[225,512]{1,0:T(8,128)S(1)} %get-tuple-element.5) | copy-start | bytes 1382404
  90.7 20.9 %copy-start.2 = (f32[225,512]{1,0:T(8,128)}, f32[225,512]{1,0:T(8,128)S(1)}, u32[]{:S(2)}) copy-start(f32[225,512]{1,0:T(8,128)S(1)} %get-tuple-element.6) | copy-start | bytes 1382404
  115.4 4.2 %copy-start.4 = (s32[2]{0:T(128)S(1)}, s32[2]{0:T(128)}, u32[]{:S(2)}) copy-start(s32[2]{0:T(128)} %param.11) | copy-start | bytes 28
  115.4 44.0 %all-to-all-start.1 = ((f32[32,6,2,1024]{3,2,1,0:T(2,128)}), f32[32,6,2,1024]{3,2,1,0:T(2,128)S(1)}, u32[]{:S(2)}, u32[]{:S(2)}) async-start(f32[32,6,2,1024]{3,2,1,0:T(2,128)} %copy.44), calls=%async_computation.1 | async-start | bytes 3145728 | tf_op jit(solution)/shard_map/all_to_all | solution.py:34
  161.8 45.6 %all-to-all-start.2 = ((f32[32,6,2,1024]{3,2,1,0:T(2,128)}), f32[32,6,2,1024]{3,2,1,0:T(2,128)S(1)}, u32[]{:S(2)}, u32[]{:S(2)}) async-start(f32[32,6,2,1024]{3,2,1,0:T(2,128)} %broadcast_in_dim.47), calls=%async_computation.2 | async-start | bytes 3145728 | tf_op jit(solution)/shard_map/all_to_all | solution.py:46
where the time goes:
time: 213 us; the launch traced here: 212 us
  waiting for transfers between devices  84.4 us (40%)
  blocking collectives  68.8 us (32%)
  other arithmetic  16.4 us (8%)
  starting transfers between devices  15.7 us (7%)
  local copies, waits for them, and re-layouts  14.6 us (7%)
  matrix products  11.7 us (5%)
    all_to_all x1, blocking collectives, local(): lax.all_to_all(outgoing, 'col', split_axis=1, concat_axis=1, tiled=True)  68.8 us
    all_to_all x1, waiting for transfers between devices, sent_and_summed(): tiles = lax.all_to_all(cut_along(array, dim, size), axis, 0, 0, tiled=True)  39.7 us
    all_to_all x1, waiting for transfers between devices, copy_for_each(): lax.all_to_all(jnp.broadcast_to(array[None], (size, *array.shape)), axis,...  38.5 us
    convert_element_type x1, other arithmetic, local(): slot_owned = slot_rows[:, levels, 0].astype(jnp.int32)  10.3 us
    all_to_all x1, starting transfers between devices, copy_for_each(): lax.all_to_all(jnp.broadcast_to(array[None], (size, *array.shape)), axis,...  5.81 us
    dot_general x1, matrix products, local(): jnp.einsum('lnb,nbt->nlt', picked, weights, preferred_element_type=jnp.fl...  4.73 us
  transfers between devices with their start and end apart: 4, of which 4 were waited for; matrix products, arithmetic and copies ran while one was open for 2% of the time, Pallas kernels for 0%

commit v1 on v0

v1 whole, which is shorter than its diff:
```python
import functools
import math

import jax
import jax.numpy as jnp
from jax import lax
from jax.experimental import pallas as pl
from jax.experimental.pallas import tpu as pltpu
from jax.sharding import PartitionSpec as P

NLON = 7200
KW = 512
CAP = 6
ROWS = 40
SENT = 37
TWO_PI = 6.283185307179586
MESH = pl.DeviceIdType.MESH
F32 = jnp.float32
BF16 = jnp.bfloat16
NZ, NX = 8, 4


def real_dft(xs):
    n = len(xs)
    if n == 1:
        return [(xs[0], None)]
    if n == 2:
        return [(xs[0] + xs[1], None), (xs[0] - xs[1], None)]
    even, odd = real_dft(xs[0::2]), real_dft(xs[1::2])
    half = n // 2

    def entry(spec, r):
        if r <= half // 2:
            re, im = spec[r]
            return re, im
        re, im = spec[half - r]
        return re, (None if im is None else -im)

    out = []
    for r in range(half + 1):
        if r == half:
            out.append((even[0][0] - odd[0][0], None))
            continue
        er, ei = entry(even, r)
        o_r, oi = entry(odd, r)
        if r == 0:
            out.append((er + o_r, None))
            continue
        if 4 * r == n:
            re = er if oi is None else er + oi
            im = -o_r if ei is None else ei - o_r
            out.append((re, im))
            continue
        c, s = math.cos(2 * math.pi * r / n), math.sin(2 * math.pi * r / n)
        if oi is None:
            tr, ti = c * o_r, -s * o_r
        else:
            tr, ti = c * o_r + s * oi, c * oi - s * o_r
        out.append((er + tr, ti if ei is None else ei + ti))
    return out


def real_idft(hs, n):
    if n == 1:
        return [hs[0][0]]
    if n == 2:
        return [hs[0][0] + hs[1][0], hs[0][0] - hs[1][0]]
    half = n // 2
    evens, odds = [], []
    for r in range(half // 2 + 1):
        re, im = hs[r]
        mr, mi = hs[half - r]
        sum_re, dif_re = re + mr, re - mr
        if r == 0:
            evens.append((sum_re, None))
            odds.append((dif_re, None))
            continue
        if 2 * r == half:
            evens.append((sum_re, None))
            odds.append((-2.0 * im, None))
            continue
        sum_im, dif_im = im - mi, im + mi
        c, s = math.cos(2 * math.pi * r / n), math.sin(2 * math.pi * r / n)
        evens.append((sum_re, sum_im))
        odds.append((c * dif_re - s * dif_im, c * dif_im + s * dif_re))
    a, b = real_idft(evens, half), real_idft(odds, half)
    out = []
    for x, y in zip(a, b):
        out += [x, y]
    return out


def halves(x):
    hi = x.astype(BF16)
    return hi, (x - hi.astype(F32)).astype(BF16)


def fill_tables(base_ref, table):
    ca, sa = base_ref[0:16, :], base_ref[16:32, :]
    for r in range(17):
        parts = []
        for k, sign in ((r, 1.0), (32 - r, -1.0)):
            cb = base_ref[32 + k : 33 + k, :]
            sb = base_ref[72 + k : 73 + k, :]
            c = ca * cb - sa * sb
            s = sa * cb + ca * sb
            parts.append((c, s, sign))
        for p, (c, s, sign) in enumerate(parts):
            for row, half, value in (
                (32 * p, 0, c),
                (32 * p, 1, sign * s),
                (32 * p + 16, 0, -s),
                (32 * p + 16, 1, sign * c),
            ):
                hi, lo = halves(value)
                table[0, r, row : row + 16, 256 * half : 256 * half + 256] = hi
                table[1, r, row : row + 16, 256 * half : 256 * half + 256] = lo


def zonal(rows_ref, out_ref, table, scale_ref):
    spec = real_dft([rows_ref[c] for c in range(32)])
    nt = (((1,), (1,)), ((), ()))
    nn = (((1,), (0,)), ((), ()))

    def widen(y):
        v0, v1, v2 = y[0:8], y[8:16], y[16:24]
        rolled = jnp.concatenate([v1[4:8], v1[0:4]], axis=0)
        return jnp.concatenate(
            [jnp.concatenate([v0, v1], axis=0), jnp.concatenate([v2, rolled], axis=0)], axis=1
        )

    def narrow(w):
        a, b = w[:, 0:128], w[:, 128:256]
        mid = jnp.concatenate([a[8:12], b[8:12]], axis=0)
        return jnp.concatenate([a[0:8], mid, b[0:8]], axis=0)

    back = []
    for r in range(17):
        re, im = spec[r]
        re = widen(re)
        im = jnp.zeros_like(re) if im is None else widen(im)
        hi, lo = halves(jnp.concatenate([re, im], axis=1))
        both = jnp.concatenate([hi, lo], axis=0)
        p = lax.dot_general(both, table[0, r], nt, preferred_element_type=F32)
        q = lax.dot_general(hi, table[1, r], nt, preferred_element_type=F32)
        s = (p[0:16] + p[16:32] + q) * scale_ref[r]
        hi, lo = halves(s)
        both = jnp.concatenate([hi, lo], axis=0)
        p = lax.dot_general(both, table[0, r], nn, preferred_element_type=F32)
        q = lax.dot_general(hi, table[1, r], nn, preferred_element_type=F32)
        w = p[0:16] + p[16:32] + q
        back.append((narrow(w[:, 0:256]), None if r in (0, 16) else narrow(w[:, 256:512])))
    for c, value in enumerate(real_idft(back, 32)):
        out_ref[c] = value


def exchange_kernel(sb_ref, id_ref, part_ref, out_ref, send, recv, data, send_sem, recv_sem):
    bands = lax.axis_size("band")
    band, col = lax.axis_index("band"), lax.axis_index("col")
    z, x = col // NX, lax.rem(col, NX)
    cols = NZ * NX

    def peer(i):
        u, dx = i // NX, lax.rem(i, NX)
        m = (u + 1) // 2
        dz = jnp.where(lax.rem(u, 2) == 0, 4 + m, 4 - m)
        return lax.rem(z + dz, NZ) * NX + lax.rem(x + dx, NX)

    def targets(act):
        def step(i, carry):
            to = peer(i)
            for off in (0, 2, 1):
                other = band + off - 1
                if off == 1:
                    ok = to != col
                else:
                    ok = (other >= 0) & (other < bands)

                @pl.when(ok)
                def _(off=off, other=other):
                    act(off, other, to)

            return carry

        lax.fori_loop(0, cols, step, 0)

    barrier = pltpu.get_barrier_semaphore()
    targets(lambda off, b, c: pl.semaphore_signal(barrier, inc=1, device_id=(b, c), device_id_type=MESH))

    for side, edge in ((0, 0), (2, bands - 1)):

        @pl.when(band == edge)
        def _(side=side):
            recv[side] = jnp.full(recv.shape[1:], -1.0, F32)

    def pack(j, carry):
        off, c = j // cols, lax.rem(j, cols)
        for s in range(CAP):
            block = sb_ref[j * CAP + s]
            send[off, c, pl.ds(s, 6, stride=CAP), :] = part_ref[block]
        send[off, c, 36:37, :] = id_ref[pl.ds(j, 1), :]
        return carry

    lax.fori_loop(0, 3 * cols, pack, 0)
    inner = (band > 0).astype(jnp.int32) + (band < bands - 1).astype(jnp.int32)
    pl.semaphore_wait(barrier, cols - 1 + cols * inner)

    def start(off, b, c):
        pltpu.make_async_remote_copy(
            src_ref=send.at[off, c, 0:SENT],
            dst_ref=recv.at[2 - off, col, 0:SENT],
            send_sem=send_sem.at[off],
            recv_sem=recv_sem.at[2 - off],
            device_id=(b, c),
            device_id_type=MESH,
        ).start()

    targets(start)
    own = pltpu.make_async_copy(send.at[1, col, 0:SENT], recv.at[1, col, 0:SENT], recv_sem.at[1])
    own.start()
    data[...] = jnp.zeros_like(data)

    def drain(off):
        pltpu.make_async_copy(recv.at[off, :, 0:SENT], recv.at[off, :, 0:SENT], recv_sem.at[off]).wait()

    def drain_send(off, n):
        pltpu.make_async_copy(
            send.at[off, 0:n, 0:SENT], send.at[off, 0:n, 0:SENT], send_sem.at[off]
        ).wait()

    drain(1)
    drain_send(1, cols - 1)
    for off in (0, 2):
        other = band + off - 1

        @pl.when((other >= 0) & (other < bands))
        def _(off=off):
            drain(off)
            drain_send(off, cols)

    for off in range(3):

        def lay(c, carry, off=off):
            j = off * cols + c
            for lev in range(6):
                data[pl.ds(pl.multiple_of(j * 8, 8), 6), 128 * lev : 128 * lev + 128] = recv[
                    off, c, lev * CAP : lev * CAP + CAP, :
                ]
            return carry

        lax.fori_loop(0, cols, lay, 0)
    ids = recv[:, :, 36:37, :].reshape(3 * cols, 1, 128)
    lane = lax.broadcasted_iota(jnp.int32, (3 * cols, 8, 128), 2)
    sub = lax.broadcasted_iota(jnp.int32, (3 * cols, 8, 128), 1)
    diag = jnp.where(lane == sub, jnp.broadcast_to(ids, (3 * cols, 8, 128)), 0.0)
    diag = diag.reshape(24 * cols, 128).astype(BF16)
    spread = jnp.dot(diag, jnp.ones((128, 128), BF16), preferred_element_type=F32)
    tile = lax.broadcasted_iota(jnp.int32, (24 * cols, 128), 1).astype(F32)
    chooser = (spread == tile).astype(F32).astype(BF16)
    hi, lo = halves(data[...])
    tn = (((0,), (0,)), ((), ()))
    out_ref[...] = lax.dot_general(chooser, hi, tn, preferred_element_type=F32) + lax.dot_general(
        chooser, lo, tn, preferred_element_type=F32
    )


def zonal_kernel(base_ref, scale_ref, rows_ref, out_ref, table):
    fill_tables(base_ref, table)
    zonal(rows_ref, out_ref, table, scale_ref)


def base_tables():
    i = lax.broadcasted_iota(jnp.int32, (112, 256), 1)
    row = lax.broadcasted_iota(jnp.int32, (112, 256), 0)
    k = jnp.where(row < 32, 32 * (row % 16), (row - 32) % 40)
    angle = ((i * k) % NLON).astype(F32) * (TWO_PI / NLON)
    is_sin = ((row >= 16) & (row < 32)) | (row >= 72)
    value = jnp.where(is_sin, jnp.sin(angle), jnp.cos(angle))
    return jnp.where(i < 225, value, 0.0)


def scales(cutoff):
    r = lax.broadcasted_iota(jnp.int32, (17, 16, 64), 0)
    row = lax.broadcasted_iota(jnp.int32, (17, 16, 64), 1)
    n = lax.broadcasted_iota(jnp.int32, (17, 16, 64), 2)
    mirror = n >= 32
    k = 32 * (n % 16) + jnp.where(mirror, 32 - r, r)
    used = (~mirror) | ((r > 0) & (r < 16))
    weight = jnp.where((k > 0) & ((r == 0) | (r == 16)), 2.0, 1.0) / NLON
    limit = jnp.where(row < 6, cutoff[0], cutoff[1])
    return jnp.where(used & (k <= limit), weight, 0.0).astype(F32)


def to_chunk(a):
    a = jnp.pad(a.reshape(32, 12, 225), ((0, 0), (0, 0), (0, 31)))
    first, second = a[:, :, :128], a[:, :, 128:]
    return jnp.concatenate([first, second[:, 8:12], second[:, 0:8]], axis=1)


def from_chunk(a):
    second = jnp.concatenate([a[:, 16:24], a[:, 12:16]], axis=1)
    return jnp.concatenate([a[:, :12], second], axis=2)[:, :, :225].reshape(32, 2, 6, 225)


def local(source, weights, source_block, owner_device, target_tile, cutoff):
    cols = lax.axis_size("col")
    levels, nb, width = 6, weights.shape[0], weights.shape[1]
    band = lax.axis_index("band")
    picked = jnp.take(source.reshape(levels, -1, width), source_block, axis=1)
    partial = jnp.einsum("lnb,nbt->nlt", picked, weights, preferred_element_type=F32)
    owners = owner_device[:, 0]
    row = lax.broadcasted_iota(jnp.int32, (nb, nb), 0)
    column = lax.broadcasted_iota(jnp.int32, (nb, nb), 1)
    earlier = (owners[None, :] == owners[:, None]) & (column < row)
    rank = jnp.sum(earlier.astype(jnp.int32), axis=1)
    slot = (owners - (band - 1) * cols) * CAP + rank
    total = 3 * cols * CAP
    hit = lax.broadcasted_iota(jnp.int32, (total, nb), 0) == slot[None, :]
    both = jnp.arange(nb, dtype=jnp.int32) * 128 + target_tile
    code = jnp.sum(jnp.where(hit, both[None, :] + 1, 0), axis=1)
    sb = jnp.maximum(code - 1, 0) // 128
    tid = jnp.where(code > 0, (code - 1) % 128, -1).astype(F32)
    id_rows = jnp.pad(tid.reshape(3 * cols, CAP), ((0, 0), (0, 128 - CAP)), constant_values=-1.0)
    vmem = pl.BlockSpec(memory_space=pltpu.VMEM)
    summed = pl.pallas_call(
        exchange_kernel,
        name="exchange",
        out_shape=jax.ShapeDtypeStruct((128, 768), F32),
        in_specs=[pl.BlockSpec(memory_space=pltpu.SMEM), vmem, vmem],
        out_specs=vmem,
        scratch_shapes=[
            pltpu.VMEM((3, cols, ROWS, 128), F32),
            pltpu.VMEM((3, cols, ROWS, 128), F32),
            pltpu.VMEM((24 * cols, 768), F32),
            pltpu.SemaphoreType.DMA((3,)),
            pltpu.SemaphoreType.DMA((3,)),
        ],
        compiler_params=pltpu.CompilerParams(
            collective_id=0, has_side_effects=True, vmem_limit_bytes=50 * 2**20
        ),
    )(sb, id_rows, partial)
    flat = jnp.transpose(summed[:113].reshape(113, 6, 128), (1, 0, 2)).reshape(6, 113 * 128)
    remapped = flat[:, :14400].reshape(6, 64, 225)
    out_rows = to_chunk(jnp.transpose(remapped.reshape(6, 32, 2, 225), (1, 2, 0, 3)))
    rows = lax.all_to_all(out_rows, "col", 0, 0, tiled=True)
    back = pl.pallas_call(
        zonal_kernel,
        name="zonal",
        out_shape=jax.ShapeDtypeStruct((32, 24, 128), F32),
        in_specs=[vmem, vmem, vmem],
        out_specs=vmem,
        scratch_shapes=[pltpu.VMEM((2, 17, 64, 512), BF16)],
        compiler_params=pltpu.CompilerParams(vmem_limit_bytes=50 * 2**20),
    )(base_tables(), scales(cutoff), rows)
    filtered = from_chunk(lax.all_to_all(back, "col", 0, 0, tiled=True))
    filtered = jnp.transpose(filtered, (2, 0, 1, 3)).reshape(6, 64, 225)
    return remapped, filtered


def solution(mesh):
    in_specs = (
        P(None, ("band", "col")),
        P(("band", "col"), None, None),
        P(("band", "col")),
        P(("band", "col"), None),
        P(("band", "col")),
        P(("band", "col")),
    )
    out_specs = (P(None, "band", "col"), P(None, "band", "col"))
    return jax.shard_map(local, mesh=mesh, in_specs=in_specs, out_specs=out_specs, check_vma=False)
```

time: 213 us -> 115 us (0.54)
  blocking collectives: 68.8 us -> 0 us
  Pallas kernels: 0 us -> 59.9 us
  waiting for transfers between devices: 84.4 us -> 26.1 us
  other arithmetic: 16.4 us -> 6.18 us
  local copies, waits for them, and re-layouts: 14.6 us -> 5.94 us
  matrix products: 11.7 us -> 4.73 us
  starting transfers between devices: 15.7 us -> 10.7 us
    all_to_all x1 -> x0, blocking collectives: 68.8 us -> none  [local(): lax.all_to_all(outgoing, 'col', split_axis=1, concat_axis=1, tiled=True)]
    pallas_call x0 -> x2, Pallas kernels: none -> 59.9 us  [the longest x1 55.5 us: local(): pl.pallas_call(exchange_kernel, name='exchange', out_shape=jax.ShapeDtype...]
    all_to_all x2, waiting for transfers between devices: 78.3 us -> 26.1 us  [the longest x1 13.5 us: local(): filtered = from_chunk(lax.all_to_all(back, 'col', 0, 0, tiled=True))]
    convert_element_type x2 -> x1, other arithmetic: 11 us -> 0.03 us  [local(): tid = jnp.where(code > 0, (code - 1) % 128, -1).astype(F32)]
    dot_general x5 -> x1, matrix products: 11.7 us -> 4.73 us  [local(): jnp.einsum('lnb,nbt->nlt', picked, weights, preferred_element_type=F32)]
    ppermute x2 -> x0, waiting for transfers between devices: 6.12 us -> none  [the longest x1 3.42 us: extended(): before = lax.ppermute(last, axis, up)]
    ppermute x2 -> x0, starting transfers between devices: 5.73 us -> none  [the longest x1 3.81 us: extended(): after = lax.ppermute(leading, axis, down)]
    dot_general x4 -> x0, local copies, waits for them, and re-layouts: 3.26 us -> none  [the longest x1 1.22 us: local(): jnp.dot(placing.astype(jnp.float32), tagged.reshape(block_count, (levels...]
  transfers between devices with their start and end apart: 4 -> 2, of which waited for: 4 -> 2; matrix products, arithmetic and copies ran while one was open for 2% -> 3% of each run, Pallas kernels for 0% -> 0%
where the time goes in v1:
time: 115 us; the launch traced here: 114 us
  Pallas kernels  59.9 us (52%)
  waiting for transfers between devices  26.1 us (23%)
  starting transfers between devices  10.7 us (9%)
  other arithmetic  6.18 us (5%)
  local copies, waits for them, and re-layouts  5.94 us (5%)
  matrix products  4.73 us (4%)
    pallas_call x1, Pallas kernels, local(): pl.pallas_call(exchange_kernel, name='exchange', out_shape=jax.ShapeDtype...  55.5 us
    all_to_all x1, waiting for transfers between devices, local(): filtered = from_chunk(lax.all_to_all(back, 'col', 0, 0, tiled=True))  13.5 us
    all_to_all x1, waiting for transfers between devices, local(): rows = lax.all_to_all(out_rows, 'col', 0, 0, tiled=True)  12.6 us
    all_to_all x1, starting transfers between devices, local(): rows = lax.all_to_all(out_rows, 'col', 0, 0, tiled=True)  6.42 us
    dot_general x1, matrix products, local(): jnp.einsum('lnb,nbt->nlt', picked, weights, preferred_element_type=F32)  4.73 us
    pallas_call x1, Pallas kernels, local(): pl.pallas_call(zonal_kernel, name='zonal', out_shape=jax.ShapeDtypeStruct...  4.42 us
    all_to_all x1, starting transfers between devices, local(): filtered = from_chunk(lax.all_to_all(back, 'col', 0, 0, tiled=True))  4.3 us
  transfers between devices with their start and end apart: 2, of which 2 were waited for; matrix products, arithmetic and copies ran while one was open for 3% of the time, Pallas kernels for 0%

profile of v1, /device:TPU:16, one launch (start us, length us, event | category | flops | bytes accessed | tf_op | source)
XLA Modules:
  0.0 114.5 jit_solution(4773946633314383306)
XLA Ops:
  0.6 0.9 convert_reduce_fusion
  1.6 0.7 add_add_fusion
  2.3 0.2 select_reduce_fusion
  2.5 0.7 compare_select_fusion
  3.2 0.7 compare_and_fusion.4
  4.2 0.8 gather_fusion
  5.1 4.7 %fusion.part_ref = f32[256,6,128]{2,1,0:T(8,128)S(1)} fusion(bf16[256,128,128]{2,1,0:T(8,128)(2,1)} %param.7, bf16[256,6,128]{2,1,0:T(8,128)(2,1)S(1)} %gather_fusion, pred[256]{0:T(512)(128)(4,1)S(1)} %compare_and_fusion.4), kind=kOutput, calls=%fused_computation.5 | convolution fusion | flops 50528256 | bytes 9568512 | tf_op jit(solution)/shard_map/lnb,nbt->nlt/dot_general | solution.py:310
  9.8 55.5 %exchange.1 = f32[128,768]{1,0:T(8,128)S(1)} custom-call(s32[576]{0:T(1024)S(1)} %get-tuple-element.3.sb_ref, f32[96,128]{1,0:T(8,128)S(1)} %pad.8.id_ref, f32[256,6,128]{2,1,0:T(8,128)S(1)} %fusion.part_ref), custom_call_target="tpu_custom_call" | custom-call | tf_op jit(solution)/shard_map/exchange/pallas_call | solution.py:325
  65.5 0.2 copy.22
  65.8 0.6 reshape_reshape.3
  66.4 0.2 copy.24
  66.8 0.8 pad_maximum_fusion.2
  67.6 6.4 %all-to-all-start = ((f32[32,24,128]{2,1,0:T(8,128)}), f32[32,24,128]{2,1,0:T(8,128)S(1)}, u32[]{:S(2)}, u32[]{:S(2)}) async-start(f32[32,24,128]{2,1,0:T(8,128)} %pad_maximum_fusion.2), calls=%async_computation | async-start | bytes 786432 | tf_op jit(solution)/shard_map/all_to_all | solution.py:345
  74.1 0.6 fusion.22
  74.7 1.3 %compare_select_fusion.1 = s32[16]{0:T(128)S(1)} fusion(s32[]{:T(128)} %bitcast.6, s32[]{:T(128)} %bitcast.5), kind=kLoop, calls=%fused_computation.46 | loop fusion | flops 32 | bytes 72 | tf_op jit(solution)/shard_map/jit(_where)/select_n | solution.py:290
  76.0 0.6 select_select_fusion.base_ref
  76.8 12.6 %all-to-all-done.rows_ref = f32[32,24,128]{2,1,0:T(8,128)S(1)} async-done(((f32[32,24,128]{2,1,0:T(8,128)}), f32[32,24,128]{2,1,0:T(8,128)S(1)}, u32[]{:S(2)}, u32[]{:S(2)}) %all-to-all-start) | async-done | bytes 393248 | tf_op jit(solution)/shard_map/all_to_all | solution.py:345
  89.4 4.4 %zonal.1 = f32[32,24,128]{2,1,0:T(8,128)} custom-call(f32[112,256]{1,0:T(8,128)S(1)} %select_select_fusion.base_ref, f32[17,16,64]{2,1,0:T(8,128)S(1)} %multiply_select_fusion.scale_ref, f32[32,24,128]{2,1,0:T(8,128)S(1)} %all-to-all-done.rows_ref), custom_call_target="tpu_custom_call" | custom-call | tf_op jit(solution)/shard_map/zonal/pallas_call | solution.py:346
  93.8 4.3 %all-to-all-start.1 = ((f32[32,24,128]{2,1,0:T(8,128)}), f32[32,24,128]{2,1,0:T(8,128)S(1)}, u32[]{:S(2)}, u32[]{:S(2)}) async-start(f32[32,24,128]{2,1,0:T(8,128)} %zonal.1), calls=%async_computation.1 | async-start | bytes 786432 | tf_op jit(solution)/shard_map/all_to_all | solution.py:355
  98.1 1.2 %reshape.51 = f32[6,64,225]{2,1,0:T(8,128)} reshape(f32[6,14400]{1,0:T(8,128)S(1)} %bitcast.23) | data formatting | bytes 691200 | tf_op jit(solution)/shard_map/reshape | solution.py:343
  99.3 13.5 %all-to-all-done.1 = f32[32,24,128]{2,1,0:T(8,128)S(1)} async-done(((f32[32,24,128]{2,1,0:T(8,128)}), f32[32,24,128]{2,1,0:T(8,128)S(1)}, u32[]{:S(2)}, u32[]{:S(2)}) %all-to-all-start.1) | async-done | bytes 393248 | tf_op jit(solution)/shard_map/all_to_all | solution.py:355
  112.9 0.2 copy.26
  113.2 0.3 copy.27
  113.5 1.0 reshape.54
  (33 shorter events, 1.0 us)
Async XLA Ops:
  0.6 3.6 %copy-start = (bf16[6,16384]{1,0:T(8,128)(2,1)S(1)}, bf16[6,16384]{1,0:T(8,128)(2,1)}, u32[]{:S(2)}) copy-start(bf16[6,16384]{1,0:T(8,128)(2,1)} %param.6) | copy-start | bytes 589828
  5.0 69.0 %copy-start.1 = (s32[2]{0:T(128)S(1)}, s32[2]{0:T(128)}, u32[]{:S(2)}) copy-start(s32[2]{0:T(128)} %param.11) | copy-start | bytes 28
  67.6 21.8 %all-to-all-start = ((f32[32,24,128]{2,1,0:T(8,128)}), f32[32,24,128]{2,1,0:T(8,128)S(1)}, u32[]{:S(2)}, u32[]{:S(2)}) async-start(f32[32,24,128]{2,1,0:T(8,128)} %pad_maximum_fusion.2), calls=%async_computation | async-start | bytes 786432 | tf_op jit(solution)/shard_map/all_to_all | solution.py:345
  93.8 19.0 %all-to-all-start.1 = ((f32[32,24,128]{2,1,0:T(8,128)}), f32[32,24,128]{2,1,0:T(8,128)S(1)}, u32[]{:S(2)}, u32[]{:S(2)}) async-start(f32[32,24,128]{2,1,0:T(8,128)} %zonal.1), calls=%async_computation.1 | async-start | bytes 786432 | tf_op jit(solution)/shard_map/all_to_all | solution.py:355

commit v2 on v1

--- a/solution.py
+++ b/solution.py
@@ -18,6 +18,7 @@
 F32 = jnp.float32
 BF16 = jnp.bfloat16
 NZ, NX = 8, 4
+GROUP = 32
 
 
 def real_dft(xs):
@@ -117,7 +118,22 @@
                 table[1, r, row : row + 16, 256 * half : 256 * half + 256] = lo
 
 
-def zonal(rows_ref, out_ref, table, scale_ref):
+def scale_at(r, cut_ref):
+    row = lax.broadcasted_iota(jnp.int32, (16, 64), 0)
+    n = lax.broadcasted_iota(jnp.int32, (16, 64), 1)
+    mirror = n >= 32
+    k = 32 * (n & 15) + jnp.where(mirror, 32 - r, r)
+    limit = jnp.where(row < 6, cut_ref[0], cut_ref[1])
+    keep = k <= limit
+    if r in (0, 16):
+        keep = keep & (n < 32)
+        weight = jnp.where(k > 0, 2.0 / NLON, 1.0 / NLON)
+    else:
+        weight = 1.0 / NLON
+    return jnp.where(keep, weight, 0.0).astype(F32)
+
+
+def zonal(rows_ref, out_ref, table, cut_ref):
     spec = real_dft([rows_ref[c] for c in range(32)])
     nt = (((1,), (1,)), ((), ()))
     nn = (((1,), (0,)), ((), ()))
@@ -143,7 +159,7 @@
         both = jnp.concatenate([hi, lo], axis=0)
         p = lax.dot_general(both, table[0, r], nt, preferred_element_type=F32)
         q = lax.dot_general(hi, table[1, r], nt, preferred_element_type=F32)
-        s = (p[0:16] + p[16:32] + q) * scale_ref[r]
+        s = (p[0:16] + p[16:32] + q) * scale_at(r, cut_ref)
         hi, lo = halves(s)
         both = jnp.concatenate([hi, lo], axis=0)
         p = lax.dot_general(both, table[0, r], nn, preferred_element_type=F32)
@@ -154,11 +170,38 @@
         out_ref[c] = value
 
 
-def exchange_kernel(sb_ref, id_ref, part_ref, out_ref, send, recv, data, send_sem, recv_sem):
+def fill_base(base):
+    for start, count, step in ((0, 16, 32), (32, 40, 1)):
+        i = lax.broadcasted_iota(jnp.int32, (count, 256), 1)
+        k = lax.broadcasted_iota(jnp.int32, (count, 256), 0) * step
+        product = (i * k).astype(F32)
+        turns = jnp.floor(product * (1.0 / NLON))
+        phase = product - turns * NLON
+        phase = jnp.where(phase < 0, phase + NLON, phase)
+        phase = jnp.where(phase >= NLON, phase - NLON, phase)
+        angle = phase * (TWO_PI / NLON)
+        base[start : start + count, :] = jnp.where(i < 225, jnp.cos(angle), 0.0)
+        base[start + count : start + 2 * count, :] = jnp.where(i < 225, jnp.sin(angle), 0.0)
+
+
+def kernel(
+    pick_ref, sb_ref, cut_ref, id_ref, src_ref, w_ref, remap_ref, filt_ref,
+    wbuf, part, send, recv, data, tiles, flat, rtx, rrx, ztx, zrx, base, table,
+    w_sem, send_sem, recv_sem, row_sem,
+):
     bands = lax.axis_size("band")
     band, col = lax.axis_index("band"), lax.axis_index("col")
     z, x = col // NX, lax.rem(col, NX)
     cols = NZ * NX
+
+    def weight_copy(g):
+        return pltpu.make_async_copy(
+            w_ref.at[pl.ds(g * GROUP, GROUP)], wbuf.at[pl.ds(g * GROUP, GROUP)], w_sem.at[g]
+        )
+
+    groups = wbuf.shape[0] // GROUP
+    for g in range(groups):
+        weight_copy(g).start()
 
     def peer(i):
         u, dx = i // NX, lax.rem(i, NX)
@@ -193,11 +236,22 @@
         def _(side=side):
             recv[side] = jnp.full(recv.shape[1:], -1.0, F32)
 
+    for g in range(groups):
+        weight_copy(g).wait()
+
+        def some(i, carry, g=g):
+            first = g * GROUP + i * 8
+            for n in range(8):
+                k = first + n
+                part[k] = jnp.dot(src_ref[pick_ref[k]], wbuf[k], preferred_element_type=F32)
+            return carry
+
+        lax.fori_loop(0, GROUP // 8, some, 0)
+
     def pack(j, carry):
         off, c = j // cols, lax.rem(j, cols)
         for s in range(CAP):
-            block = sb_ref[j * CAP + s]
-            send[off, c, pl.ds(s, 6, stride=CAP), :] = part_ref[block]
+            send[off, c, pl.ds(s, 6, stride=CAP), :] = part[sb_ref[j * CAP + s]]
         send[off, c, 36:37, :] = id_ref[pl.ds(j, 1), :]
         return carry
 
@@ -216,9 +270,10 @@
         ).start()
 
     targets(start)
-    own = pltpu.make_async_copy(send.at[1, col, 0:SENT], recv.at[1, col, 0:SENT], recv_sem.at[1])
-    own.start()
+    pltpu.make_async_copy(send.at[1, col, 0:SENT], recv.at[1, col, 0:SENT], recv_sem.at[1]).start()
     data[...] = jnp.zeros_like(data)
+    fill_base(base)
+    fill_tables(base, table)
 
     def drain(off):
         pltpu.make_async_copy(recv.at[off, :, 0:SENT], recv.at[off, :, 0:SENT], recv_sem.at[off]).wait()
@@ -229,14 +284,12 @@
         ).wait()
 
     drain(1)
-    drain_send(1, cols - 1)
     for off in (0, 2):
         other = band + off - 1
 
         @pl.when((other >= 0) & (other < bands))
         def _(off=off):
             drain(off)
-            drain_send(off, cols)
 
     for off in range(3):
 
@@ -259,55 +312,92 @@
     chooser = (spread == tile).astype(F32).astype(BF16)
     hi, lo = halves(data[...])
     tn = (((0,), (0,)), ((), ()))
-    out_ref[...] = lax.dot_general(chooser, hi, tn, preferred_element_type=F32) + lax.dot_general(
+    total = lax.dot_general(chooser, hi, tn, preferred_element_type=F32) + lax.dot_general(
         chooser, lo, tn, preferred_element_type=F32
     )
-
-
-def zonal_kernel(base_ref, scale_ref, rows_ref, out_ref, table):
-    fill_tables(base_ref, table)
-    zonal(rows_ref, out_ref, table, scale_ref)
-
-
-def base_tables():
-    i = lax.broadcasted_iota(jnp.int32, (112, 256), 1)
-    row = lax.broadcasted_iota(jnp.int32, (112, 256), 0)
-    k = jnp.where(row < 32, 32 * (row % 16), (row - 32) % 40)
-    angle = ((i * k) % NLON).astype(F32) * (TWO_PI / NLON)
-    is_sin = ((row >= 16) & (row < 32)) | (row >= 72)
-    value = jnp.where(is_sin, jnp.sin(angle), jnp.cos(angle))
-    return jnp.where(i < 225, value, 0.0)
-
-
-def scales(cutoff):
-    r = lax.broadcasted_iota(jnp.int32, (17, 16, 64), 0)
-    row = lax.broadcasted_iota(jnp.int32, (17, 16, 64), 1)
-    n = lax.broadcasted_iota(jnp.int32, (17, 16, 64), 2)
-    mirror = n >= 32
-    k = 32 * (n % 16) + jnp.where(mirror, 32 - r, r)
-    used = (~mirror) | ((r > 0) & (r < 16))
-    weight = jnp.where((k > 0) & ((r == 0) | (r == 16)), 2.0, 1.0) / NLON
-    limit = jnp.where(row < 6, cutoff[0], cutoff[1])
-    return jnp.where(used & (k <= limit), weight, 0.0).astype(F32)
-
-
-def to_chunk(a):
-    a = jnp.pad(a.reshape(32, 12, 225), ((0, 0), (0, 0), (0, 31)))
-    first, second = a[:, :, :128], a[:, :, 128:]
-    return jnp.concatenate([first, second[:, 8:12], second[:, 0:8]], axis=1)
-
-
-def from_chunk(a):
-    second = jnp.concatenate([a[:, 16:24], a[:, 12:16]], axis=1)
-    return jnp.concatenate([a[:, :12], second], axis=2)[:, :, :225].reshape(32, 2, 6, 225)
+    for lev in range(6):
+        tiles[pl.ds(lev, 128, stride=8), :] = total[:, 128 * lev : 128 * lev + 128]
+
+    for lat in range(2 * cols):
+        t, s = divmod(225 * lat, 128)
+        a, b, c = (tiles[8 * (t + n) : 8 * (t + n) + 8, :] for n in range(3))
+        if s:
+            a, b, c = (pltpu.roll(v, 128 - s, 1) for v in (a, b, c))
+            keep = lax.broadcasted_iota(jnp.int32, (8, 128), 1) < 128 - s
+            a, b = jnp.where(keep, a, b), jnp.where(keep, b, c)
+        a, b = a[0:6], b[0:6]
+        flat[pl.ds(lat, 6, stride=64), :] = a
+        flat[pl.ds(384 + lat, 6, stride=64), :] = b
+        p = lat // 2
+        if lat % 2 == 0:
+            rtx[p, 0:6, :] = a
+            rtx[p, 16:22, :] = b
+        else:
+            rtx[p, 6:12, :] = a
+            rtx[p, 22:24, :] = b[0:2]
+            rtx[p, 12:16, :] = b[2:6]
+
+    def swap(src, dst, which):
+        def step(i, carry):
+            to = peer(i)
+
+            @pl.when(to != col)
+            def _():
+                pltpu.make_async_remote_copy(
+                    src_ref=src.at[to],
+                    dst_ref=dst.at[col],
+                    send_sem=row_sem.at[which, 0],
+                    recv_sem=row_sem.at[which, 1],
+                    device_id=(band, to),
+                    device_id_type=MESH,
+                ).start()
+
+            return carry
+
+        lax.fori_loop(0, cols, step, 0)
+        pltpu.make_async_copy(src.at[col], dst.at[col], row_sem.at[which, 1]).start()
+
+    def swapped(dst, which):
+        pltpu.make_async_copy(dst, dst, row_sem.at[which, 1]).wait()
+
+    def swap_sent(src, which):
+        pltpu.make_async_copy(src.at[0 : cols - 1], src.at[0 : cols - 1], row_sem.at[which, 0]).wait()
+
+    swap(rtx, rrx, 0)
+    remap_ref[:, 0:128] = flat[0:384, :]
+    remap_ref[:, 128:225] = flat[384:768, 0:97]
+    drain_send(1, cols - 1)
+    for off in (0, 2):
+        other = band + off - 1
+
+        @pl.when((other >= 0) & (other < bands))
+        def _(off=off):
+            drain_send(off, cols)
+
+    swapped(rrx, 0)
+    zonal(rrx, ztx, table, cut_ref)
+    swap(ztx, zrx, 1)
+    swap_sent(rtx, 0)
+    swapped(zrx, 1)
+    for lat in range(2 * cols):
+        p = lat // 2
+        if lat % 2 == 0:
+            flat[pl.ds(lat, 6, stride=64), :] = zrx[p, 0:6, :]
+            flat[pl.ds(384 + lat, 6, stride=64), :] = zrx[p, 16:22, :]
+        else:
+            flat[pl.ds(lat, 6, stride=64), :] = zrx[p, 6:12, :]
+            flat[pl.ds(384 + lat, 2, stride=64), :] = zrx[p, 22:24, :]
+            flat[pl.ds(512 + lat, 4, stride=64), :] = zrx[p, 12:16, :]
+    filt_ref[:, 0:128] = flat[0:384, :]
+    filt_ref[:, 128:225] = flat[384:768, 0:97]
+    swap_sent(ztx, 1)
 
 
 def local(source, weights, source_block, owner_device, target_tile, cutoff):
     cols = lax.axis_size("col")
     levels, nb, width = 6, weights.shape[0], weights.shape[1]
     band = lax.axis_index("band")
-    picked = jnp.take(source.reshape(levels, -1, width), source_block, axis=1)
-    partial = jnp.einsum("lnb,nbt->nlt", picked, weights, preferred_element_type=F32)
+    blocks = jnp.transpose(source.reshape(levels, -1, width), (1, 0, 2))
     owners = owner_device[:, 0]
     row = lax.broadcasted_iota(jnp.int32, (nb, nb), 0)
     column = lax.broadcasted_iota(jnp.int32, (nb, nb), 1)
@@ -322,39 +412,38 @@
     tid = jnp.where(code > 0, (code - 1) % 128, -1).astype(F32)
     id_rows = jnp.pad(tid.reshape(3 * cols, CAP), ((0, 0), (0, 128 - CAP)), constant_values=-1.0)
     vmem = pl.BlockSpec(memory_space=pltpu.VMEM)
-    summed = pl.pallas_call(
-        exchange_kernel,
-        name="exchange",
-        out_shape=jax.ShapeDtypeStruct((128, 768), F32),
-        in_specs=[pl.BlockSpec(memory_space=pltpu.SMEM), vmem, vmem],
-        out_specs=vmem,
+    smem = pl.BlockSpec(memory_space=pltpu.SMEM)
+    rows = (cols, 24, 128)
+    remapped, filtered = pl.pallas_call(
+        kernel,
+        name="remap",
+        out_shape=[jax.ShapeDtypeStruct((384, 225), F32)] * 2,
+        in_specs=[smem, smem, smem, vmem, vmem, pl.BlockSpec(memory_space=pl.ANY)],
+        out_specs=[vmem, vmem],
         scratch_shapes=[
+            pltpu.VMEM((nb, width, width), BF16),
+            pltpu.VMEM((nb, 6, 128), F32),
             pltpu.VMEM((3, cols, ROWS, 128), F32),
             pltpu.VMEM((3, cols, ROWS, 128), F32),
             pltpu.VMEM((24 * cols, 768), F32),
+            pltpu.VMEM((1024, 128), F32),
+            pltpu.VMEM((768, 128), F32),
+            pltpu.VMEM(rows, F32),
+            pltpu.VMEM(rows, F32),
+            pltpu.VMEM(rows, F32),
+            pltpu.VMEM(rows, F32),
+            pltpu.VMEM((112, 256), F32),
+            pltpu.VMEM((2, 17, 64, 512), BF16),
+            pltpu.SemaphoreType.DMA((nb // GROUP,)),
             pltpu.SemaphoreType.DMA((3,)),
             pltpu.SemaphoreType.DMA((3,)),
+            pltpu.SemaphoreType.DMA((2, 2)),
         ],
         compiler_params=pltpu.CompilerParams(
             collective_id=0, has_side_effects=True, vmem_limit_bytes=50 * 2**20
         ),
-    )(sb, id_rows, partial)
-    flat = jnp.transpose(summed[:113].reshape(113, 6, 128), (1, 0, 2)).reshape(6, 113 * 128)
-    remapped = flat[:, :14400].reshape(6, 64, 225)
-    out_rows = to_chunk(jnp.transpose(remapped.reshape(6, 32, 2, 225), (1, 2, 0, 3)))
-    rows = lax.all_to_all(out_rows, "col", 0, 0, tiled=True)
-    back = pl.pallas_call(
-        zonal_kernel,
-        name="zonal",
-        out_shape=jax.ShapeDtypeStruct((32, 24, 128), F32),
-        in_specs=[vmem, vmem, vmem],
-        out_specs=vmem,
-        scratch_shapes=[pltpu.VMEM((2, 17, 64, 512), BF16)],
-        compiler_params=pltpu.CompilerParams(vmem_limit_bytes=50 * 2**20),
-    )(base_tables(), scales(cutoff), rows)
-    filtered = from_chunk(lax.all_to_all(back, "col", 0, 0, tiled=True))
-    filtered = jnp.transpose(filtered, (2, 0, 1, 3)).reshape(6, 64, 225)
-    return remapped, filtered
+    )(source_block, sb, cutoff, id_rows, blocks, weights)
+    return remapped.reshape(6, 64, 225), filtered.reshape(6, 64, 225)
 
 
 def solution(mesh):

time: 115 us -> 93.4 us (0.81)
  waiting for transfers between devices: 26.1 us -> 0 us
  Pallas kernels: 59.9 us -> 85.6 us
  starting transfers between devices: 10.7 us -> 0 us
  matrix products: 4.73 us -> 0 us
  other arithmetic: 6.18 us -> 1.86 us
  local copies, waits for them, and re-layouts: 5.94 us -> 4.06 us
    all_to_all x2 -> x0, waiting for transfers between devices: 26.1 us -> none  [the longest x1 13.5 us: local(): filtered = from_chunk(lax.all_to_all(back, 'col', 0, 0, tiled=True))]
    pallas_call x2 -> x1, Pallas kernels: 59.9 us -> 85.6 us  [local(): pl.pallas_call(kernel, name='remap', out_shape=[jax.ShapeDtypeStruct((384...]
    all_to_all x2 -> x0, starting transfers between devices: 10.7 us -> none  [the longest x1 6.42 us: local(): rows = lax.all_to_all(out_rows, 'col', 0, 0, tiled=True)]
    dot_general x1 -> x0, matrix products: 4.73 us -> none  [local(): jnp.einsum('lnb,nbt->nlt', picked, weights, preferred_element_type=F32)]
    unnamed x5 -> x8, local copies, waits for them, and re-layouts: 0.11 us -> 3.77 us
    select_n x4 -> x0, other arithmetic: 2.73 us -> none  [the longest x1 1.28 us: scales(): limit = jnp.where(row < 6, cutoff[0], cutoff[1])]
    reshape x3 -> x0, local copies, waits for them, and re-layouts: 2.46 us -> none  [the longest x1 1.2 us: local(): remapped = flat[:, :14400].reshape(6, 64, 225)]
  transfers between devices with their start and end apart: 2 -> 0, of which waited for: 2 -> 0; matrix products, arithmetic and copies ran while one was open for 3% -> 0% of each run, Pallas kernels for 0% -> 0%
where the time goes in v2:
time: 93.4 us; the launch traced here: 92.2 us
  Pallas kernels  85.6 us (92%)
  local copies, waits for them, and re-layouts  4.06 us (4%)
  other arithmetic  1.86 us (2%)
    pallas_call x1, Pallas kernels, local(): pl.pallas_call(kernel, name='remap', out_shape=[jax.ShapeDtypeStruct((384...  85.6 us
    unnamed x8, local copies, waits for them, and re-layouts  3.77 us

profile of v2, /device:TPU:16, one launch (start us, length us, event | category | flops | bytes accessed | tf_op | source)
XLA Modules:
  0.0 92.2 jit_solution(17440071286413583656)
XLA Ops:
  0.6 0.9 %convert_reduce_fusion = s32[256]{0:T(256)S(1)} fusion(s32[256]{0:T(256)} %bitcast.9), kind=kLoop, calls=%fused_computation.2 | loop fusion | flops 327424 | bytes 2048 | tf_op jit(solution)/shard_map/reduce_sum | solution.py:405
  1.6 0.7 add_add_fusion
  2.3 0.2 select_reduce_fusion
  2.5 0.2 gt.8
  2.6 0.1 sub.30
  2.8 0.0 copy-start
  2.8 0.9 %copy-done = bf16[6,16384]{1,0:T(8,128)(2,1)S(1)} copy-done((bf16[6,16384]{1,0:T(8,128)(2,1)S(1)}, bf16[6,16384]{1,0:T(8,128)(2,1)}, u32[]{:S(2)}) %copy-start) | copy-done | bytes 196632
  3.8 0.0 copy-start.1
  3.8 0.7 copy-done.1
  4.5 0.0 copy-start.2
  4.5 0.7 copy-done.2
  5.1 85.6 %remap.1 = (f32[384,225]{1,0:T(8,128)S(1)}, f32[384,225]{1,0:T(8,128)S(1)}) custom-call(s32[256]{0:T(256)S(1)} %copy-done.1, s32[576]{0:T(1024)S(1)} %get-tuple-element.7.sb_ref, s32[2]{0:T(128)S(1)} %copy-done.2, f32[96,128]{1,0:T(8,128)S(1)} %pad.4.id_ref, bf16[128,6,128]{2,1,0:T(8,128)(2,1)S(1)} %bitcast.8, bf16[256,128,128]{2,1,0:T(8,128)(2,1)} %w_ref.1), custom_call_target="tpu_custom_call" | custom-call | tf_op jit(solution)/shard_map/remap/pallas_call | solution.py:417
  90.7 0.7 copy.10
  91.5 0.7 copy.11
  (4 shorter events, 0.1 us)
Async XLA Ops:
  2.8 1.0 %copy-start = (bf16[6,16384]{1,0:T(8,128)(2,1)S(1)}, bf16[6,16384]{1,0:T(8,128)(2,1)}, u32[]{:S(2)}) copy-start(bf16[6,16384]{1,0:T(8,128)(2,1)} %param.6) | copy-start | bytes 589828
  3.8 0.7 copy-start.1
  4.5 0.7 copy-start.2

commit v3 on v2

v3 whole, which is shorter than its diff:
```python
import functools
import math

import jax
import jax.numpy as jnp
from jax import lax
from jax.experimental import pallas as pl
from jax.experimental.pallas import tpu as pltpu
from jax.sharding import PartitionSpec as P

NLON = 7200
KW = 512
CAP = 6
ROWS = 40
SENT = 37
TWO_PI = 6.283185307179586
MESH = pl.DeviceIdType.MESH
F32 = jnp.float32
BF16 = jnp.bfloat16
NZ, NX = 8, 4
GROUP = 32


def real_dft(xs):
    n = len(xs)
    if n == 1:
        return [(xs[0], None)]
    if n == 2:
        return [(xs[0] + xs[1], None), (xs[0] - xs[1], None)]
    even, odd = real_dft(xs[0::2]), real_dft(xs[1::2])
    half = n // 2

    def entry(spec, r):
        if r <= half // 2:
            re, im = spec[r]
            return re, im
        re, im = spec[half - r]
        return re, (None if im is None else -im)

    out = []
    for r in range(half + 1):
        if r == half:
            out.append((even[0][0] - odd[0][0], None))
            continue
        er, ei = entry(even, r)
        o_r, oi = entry(odd, r)
        if r == 0:
            out.append((er + o_r, None))
            continue
        if 4 * r == n:
            re = er if oi is None else er + oi
            im = -o_r if ei is None else ei - o_r
            out.append((re, im))
            continue
        c, s = math.cos(2 * math.pi * r / n), math.sin(2 * math.pi * r / n)
        if oi is None:
            tr, ti = c * o_r, -s * o_r
        else:
            tr, ti = c * o_r + s * oi, c * oi - s * o_r
        out.append((er + tr, ti if ei is None else ei + ti))
    return out


def real_idft(hs, n):
    if n == 1:
        return [hs[0][0]]
    if n == 2:
        return [hs[0][0] + hs[1][0], hs[0][0] - hs[1][0]]
    half = n // 2
    evens, odds = [], []
    for r in range(half // 2 + 1):
        re, im = hs[r]
        mr, mi = hs[half - r]
        sum_re, dif_re = re + mr, re - mr
        if r == 0:
            evens.append((sum_re, None))
            odds.append((dif_re, None))
            continue
        if 2 * r == half:
            evens.append((sum_re, None))
            odds.append((-2.0 * im, None))
            continue
        sum_im, dif_im = im - mi, im + mi
        c, s = math.cos(2 * math.pi * r / n), math.sin(2 * math.pi * r / n)
        evens.append((sum_re, sum_im))
        odds.append((c * dif_re - s * dif_im, c * dif_im + s * dif_re))
    a, b = real_idft(evens, half), real_idft(odds, half)
    out = []
    for x, y in zip(a, b):
        out += [x, y]
    return out


def halves(x):
    hi = x.astype(BF16)
    return hi, (x - hi.astype(F32)).astype(BF16)


def fill_tables(base_ref, table):
    ca, sa = base_ref[0:16, :], base_ref[16:32, :]
    for r in range(17):
        parts = []
        for k, sign in ((r, 1.0), (32 - r, -1.0)):
            cb = base_ref[32 + k : 33 + k, :]
            sb = base_ref[72 + k : 73 + k, :]
            c = ca * cb - sa * sb
            s = sa * cb + ca * sb
            parts.append((c, s, sign))
        for p, (c, s, sign) in enumerate(parts):
            for row, half, value in (
                (32 * p, 0, c),
                (32 * p, 1, sign * s),
                (32 * p + 16, 0, -s),
                (32 * p + 16, 1, sign * c),
            ):
                hi, lo = halves(value)
                table[0, r, row : row + 16, 256 * half : 256 * half + 256] = hi
                table[1, r, row : row + 16, 256 * half : 256 * half + 256] = lo


def scale_at(r, limit):
    n = lax.broadcasted_iota(jnp.int32, (8, 64), 1)
    mirror = n >= 32
    k = 32 * (n & 15) + jnp.where(mirror, 32 - r, r)
    keep = k <= limit
    if r in (0, 16):
        keep = keep & (n < 32)
        weight = jnp.where(k > 0, 2.0 / NLON, 1.0 / NLON)
    else:
        weight = 1.0 / NLON
    return jnp.where(keep, weight, 0.0).astype(F32)


def zonal(get, put, table, limit):
    spec = real_dft([get(c) for c in range(32)])
    nt = (((1,), (1,)), ((), ()))
    nn = (((1,), (0,)), ((), ()))

    def product(v, r, dims):
        hi, lo = halves(v)
        both = jnp.concatenate([hi, lo], axis=0)
        p = lax.dot_general(both, table[0, r], dims, preferred_element_type=F32)
        q = lax.dot_general(hi, table[1, r], dims, preferred_element_type=F32)
        return p[0:8] + p[8:16] + q

    back = []
    for r in range(17):
        re, im = spec[r]
        im = jnp.zeros_like(re) if im is None else im
        s = product(jnp.concatenate([re, im], axis=1), r, nt) * scale_at(r, limit)
        w = product(s, r, nn)
        back.append((w[:, 0:256], None if r in (0, 16) else w[:, 256:512]))
    for c, value in enumerate(real_idft(back, 32)):
        put(c, value)


def fill_base(base):
    for start, count, step in ((0, 16, 32), (32, 40, 1)):
        i = lax.broadcasted_iota(jnp.int32, (count, 256), 1)
        k = lax.broadcasted_iota(jnp.int32, (count, 256), 0) * step
        product = (i * k).astype(F32)
        turns = jnp.floor(product * (1.0 / NLON))
        phase = product - turns * NLON
        phase = jnp.where(phase < 0, phase + NLON, phase)
        phase = jnp.where(phase >= NLON, phase - NLON, phase)
        angle = phase * (TWO_PI / NLON)
        base[start : start + count, :] = jnp.where(i < 225, jnp.cos(angle), 0.0)
        base[start + count : start + 2 * count, :] = jnp.where(i < 225, jnp.sin(angle), 0.0)


def kernel(
    pick_ref, sb_ref, cut_ref, id_ref, src_ref, w_ref, remap_ref, filt_ref,
    wbuf, part, send, recv, data, own, dtx, drx, tiles, flat, rtx, rrx, ztx, zrx, base, table,
    w_sem, send_sem, recv_sem, dense_sem, row_sem,
):
    bands = lax.axis_size("band")
    band, col = lax.axis_index("band"), lax.axis_index("col")
    z, x = col // NX, lax.rem(col, NX)
    cols = NZ * NX
    planes = {0: (0, 1), 1: (1, 5), 2: (5, 8)}

    def weight_copy(g):
        return pltpu.make_async_copy(
            w_ref.at[pl.ds(g * GROUP, GROUP)], wbuf.at[pl.ds(g * GROUP, GROUP)], w_sem.at[g]
        )

    groups = wbuf.shape[0] // GROUP
    for g in range(groups):
        weight_copy(g).start()

    def valid(off):
        other = band + off - 1
        return (other >= 0) & (other < bands)

    barrier = pltpu.get_barrier_semaphore()

    def greet(c, carry):
        for off in (0, 1, 2):
            ok = c != col if off == 1 else valid(off)

            @pl.when(ok)
            def _(off=off):
                pl.semaphore_signal(barrier, inc=1, device_id=(band + off - 1, c), device_id_type=MESH)

        return carry

    lax.fori_loop(0, cols, greet, 0)

    for side, edge in ((0, 0), (2, bands - 1)):

        @pl.when(band == edge)
        def _(side=side):
            for d in range(NZ):
                first = d * 3 * NX + side * NX
                recv[first : first + NX] = jnp.full((NX, *recv.shape[1:]), -1.0, F32)

    for g in range(groups):
        weight_copy(g).wait()

        def some(i, carry, g=g):
            first = g * GROUP + i * 8
            for n in range(8):
                k = first + n
                part[k] = jnp.dot(src_ref[pick_ref[k]], wbuf[k], preferred_element_type=F32)
            return carry

        lax.fori_loop(0, GROUP // 8, some, 0)

    def turn(parity):
        return 1 - 2 * (parity & 1)

    def route(i, off):
        u = i // NX
        delta = jnp.where(u < 3, 5 + u, 7 - u)
        s = turn(band + off - 1)
        owner_z = lax.rem(z - s * delta + 2 * NZ, NZ)
        shift = jnp.where(delta == 0, 0, jnp.where(delta <= 4, s, -s))
        plane = lax.rem(owner_z + shift + NZ, NZ)
        to_x = lax.rem(x + i, NX)
        return owner_z * NX + to_x, delta, plane * NX + to_x

    def pack(i):
        for off in range(3):
            c, _, _ = route(i, off)
            j = off * cols + c
            for s in range(CAP):
                send[off, c, pl.ds(s, 6, stride=CAP), :] = part[sb_ref[j * CAP + s]]
            send[off, c, 36:37, :] = id_ref[pl.ds(j, 1), :]

    def transmit(i):
        for off in (0, 2, 1):
            c, delta, to = route(i, off)
            ok = to != col if off == 1 else valid(off)
            group = jnp.where(delta == 0, 0, jnp.where(delta <= 4, 1, 2))

            @pl.when(ok)
            def _(off=off, c=c, delta=delta, to=to, group=group):
                pltpu.make_async_remote_copy(
                    src_ref=send.at[off, c, 0:SENT],
                    dst_ref=recv.at[delta * 3 * NX + (2 - off) * NX + x, 0:SENT],
                    send_sem=send_sem.at[off],
                    recv_sem=recv_sem.at[group, 2 - off],
                    device_id=(band + off - 1, to),
                    device_id_type=MESH,
                ).start()

    pack(0)
    inner = (band > 0).astype(jnp.int32) + (band < bands - 1).astype(jnp.int32)
    pl.semaphore_wait(barrier, cols - 1 + cols * inner)

    def both(i, carry):
        @pl.when(i < cols - 1)
        def _():
            pack(i + 1)

        transmit(i)
        return carry

    lax.fori_loop(0, cols, both, 0)
    mine = turn(band)
    up = lax.rem(z + mine + NZ, NZ) * NX + x
    down = lax.rem(z - mine + NZ, NZ) * NX + x
    for c, delta, group in ((col, 0, 0), (down, 1, 1), (up, 7, 2)):
        pltpu.make_async_copy(
            send.at[1, c, 0:SENT],
            recv.at[delta * 3 * NX + NX + x, 0:SENT],
            recv_sem.at[group, 1],
        ).start()
    data[...] = jnp.zeros_like(data)
    fill_base(base)
    fill_tables(base, table)

    def take(group):
        first, last = planes[group]
        n = (last - first) * NX
        for off in range(3):
            wait = pltpu.make_async_copy(recv.at[0:n, 0:SENT], recv.at[0:n, 0:SENT], recv_sem.at[group, off])
            if off == 1:
                wait.wait()
            else:

                @pl.when(valid(off))
                def _(wait=wait):
                    wait.wait()

    def summed(group):
        first, last = (3 * NX * p for p in planes[group])
        n = last - first

        def lay(i, carry):
            j = first + i
            for lev in range(6):
                data[pl.ds(pl.multiple_of(j * 8, 8), 6), 128 * lev : 128 * lev + 128] = recv[
                    j, lev * CAP : lev * CAP + CAP, :
                ]
            return carry

        lax.fori_loop(0, n, lay, 0)
        ids = recv[first:last, 36:37, :].reshape(n, 1, 128)
        lane = lax.broadcasted_iota(jnp.int32, (n, 8, 128), 2)
        sub = lax.broadcasted_iota(jnp.int32, (n, 8, 128), 1)
        diag = jnp.where(lane == sub, jnp.broadcast_to(ids, (n, 8, 128)), 0.0)
        diag = diag.reshape(8 * n, 128).astype(BF16)
        spread = jnp.dot(diag, jnp.ones((128, 128), BF16), preferred_element_type=F32)
        tile = lax.broadcasted_iota(jnp.int32, (8 * n, 128), 1).astype(F32)
        chooser = (spread == tile).astype(F32).astype(BF16)
        hi, lo = halves(data[8 * first : 8 * last, :])
        tn = (((0,), (0,)), ((), ()))
        return lax.dot_general(chooser, hi, tn, preferred_element_type=F32) + lax.dot_general(
            chooser, lo, tn, preferred_element_type=F32
        )

    def dense(which, to):
        return pltpu.make_async_remote_copy(
            src_ref=dtx.at[which, :, 0:113],
            dst_ref=drx.at[which, :, 0:113],
            send_sem=dense_sem.at[which, 0],
            recv_sem=dense_sem.at[which, 1],
            device_id=(band, to),
            device_id_type=MESH,
        )

    for group, which, to in ((2, 1, up), (0, None, None), (1, 0, down)):
        take(group)
        total = summed(group)
        if which is None:
            own[...] = total
            continue
        for lev in range(6):
            dtx[which, lev] = total[0:120, 128 * lev : 128 * lev + 128]
        dense(which, to).start()

    dense(1, up).wait()
    dense(0, down).wait()
    for lev in range(6):
        tiles[pl.ds(lev, 120, stride=8), :] = (
            own[0:120, 128 * lev : 128 * lev + 128] + drx[0, lev] + drx[1, lev]
        )

    def row(lat):
        t, s = divmod(225 * lat, 128)
        a, b, c = (tiles[8 * (t + n) : 8 * (t + n) + 8, :] for n in range(3))
        if s:
            a, b, c = (pltpu.roll(v, 128 - s, 1) for v in (a, b, c))
            keep = lax.broadcasted_iota(jnp.int32, (8, 128), 1) < 128 - s
            a, b = jnp.where(keep, a, b), jnp.where(keep, b, c)
        return a[0:6], b[0:6]

    def swap(src, dst, which, j):
        def step(i, carry):
            u = i // NX
            m = (u + 1) // 2
            dz = jnp.where(lax.rem(u, 2) == 0, 4 + m, 4 - m)
            to = lax.rem(z + dz, NZ) * NX + lax.rem(x + i, NX)

            @pl.when(to != col)
            def _():
                pltpu.make_async_remote_copy(
                    src_ref=src.at[j, to, 0:12],
                    dst_ref=dst.at[j, col, 0:12],
                    send_sem=row_sem.at[which, j, 0],
                    recv_sem=row_sem.at[which, j, 1],
                    device_id=(band, to),
                    device_id_type=MESH,
                ).start()

            return carry

        lax.fori_loop(0, cols, step, 0)
        pltpu.make_async_copy(src.at[j, col, 0:12], dst.at[j, col, 0:12], row_sem.at[which, j, 1]).start()

    def swapped(dst, which, j):
        pltpu.make_async_copy(dst.at[j, :, 0:12], dst.at[j, :, 0:12], row_sem.at[which, j, 1]).wait()

    def swap_sent(src, which, j):
        part_of = src.at[j, 0 : cols - 1, 0:12]
        pltpu.make_async_copy(part_of, part_of, row_sem.at[which, j, 0]).wait()

    for j in range(2):
        for lat in range(j, 2 * cols, 2):
            a, b = row(lat)
            flat[pl.ds(lat, 6, stride=64), :] = a
            flat[pl.ds(384 + lat, 6, stride=64), :] = b
            rtx[j, lat // 2, 0:6, :] = a
            rtx[j, lat // 2, 6:12, :] = b
        swap(rtx, rrx, 0, j)
    remap_ref[:, 0:128] = flat[0:384, :]
    remap_ref[:, 128:225] = flat[384:768, 0:97]

    for j in range(2):
        swapped(rrx, 0, j)

        def get(c, j=j):
            return jnp.concatenate([rrx[j, c, 0:8, :], rrx[j, c, 6:14, :]], axis=1)

        def put(c, value, j=j):
            ztx[j, c, 0:6, :] = value[0:6, 0:128]
            ztx[j, c, 6:12, :] = value[0:6, 128:256]

        zonal(get, put, table, cut_ref[j])
        swap(ztx, zrx, 1, j)

    pltpu.make_async_copy(
        send.at[1, 0 : cols - 3, 0:SENT], send.at[1, 0 : cols - 3, 0:SENT], send_sem.at[1]
    ).wait()
    for off in (0, 2):

        @pl.when(valid(off))
        def _(off=off):
            pltpu.make_async_copy(send.at[off, :, 0:SENT], send.at[off, :, 0:SENT], send_sem.at[off]).wait()

    for j in range(2):
        swap_sent(rtx, 0, j)
    for j in range(2):
        swapped(zrx, 1, j)
        for lat in range(j, 2 * cols, 2):
            flat[pl.ds(lat, 6, stride=64), :] = zrx[j, lat // 2, 0:6, :]
            flat[pl.ds(384 + lat, 6, stride=64), :] = zrx[j, lat // 2, 6:12, :]
    filt_ref[:, 0:128] = flat[0:384, :]
    filt_ref[:, 128:225] = flat[384:768, 0:97]
    for j in range(2):
        swap_sent(ztx, 1, j)


def local(source, weights, source_block, owner_device, target_tile, cutoff):
    cols = lax.axis_size("col")
    levels, nb, width = 6, weights.shape[0], weights.shape[1]
    band = lax.axis_index("band")
    blocks = jnp.transpose(source.reshape(levels, -1, width), (1, 0, 2))
    owners = owner_device[:, 0]
    row = lax.broadcasted_iota(jnp.int32, (nb, nb), 0)
    column = lax.broadcasted_iota(jnp.int32, (nb, nb), 1)
    earlier = (owners[None, :] == owners[:, None]) & (column < row)
    rank = jnp.sum(earlier.astype(jnp.int32), axis=1)
    slot = (owners - (band - 1) * cols) * CAP + rank
    total = 3 * cols * CAP
    hit = lax.broadcasted_iota(jnp.int32, (total, nb), 0) == slot[None, :]
    both = jnp.arange(nb, dtype=jnp.int32) * 128 + target_tile
    code = jnp.sum(jnp.where(hit, both[None, :] + 1, 0), axis=1)
    sb = jnp.maximum(code - 1, 0) // 128
    tid = jnp.where(code > 0, (code - 1) % 128, -1).astype(F32)
    id_rows = jnp.pad(tid.reshape(3 * cols, CAP), ((0, 0), (0, 128 - CAP)), constant_values=-1.0)
    vmem = pl.BlockSpec(memory_space=pltpu.VMEM)
    smem = pl.BlockSpec(memory_space=pltpu.SMEM)
    rows = (2, cols, 16, 128)
    remapped, filtered = pl.pallas_call(
        kernel,
        name="remap",
        out_shape=[jax.ShapeDtypeStruct((384, 225), F32)] * 2,
        in_specs=[smem, smem, smem, vmem, vmem, pl.BlockSpec(memory_space=pl.ANY)],
        out_specs=[vmem, vmem],
        scratch_shapes=[
            pltpu.VMEM((nb, width, width), BF16),
            pltpu.VMEM((nb, 6, 128), F32),
            pltpu.VMEM((3, cols, ROWS, 128), F32),
            pltpu.VMEM((3 * cols, ROWS, 128), F32),
            pltpu.VMEM((24 * cols, 768), F32),
            pltpu.VMEM((128, 768), F32),
            pltpu.VMEM((2, 6, 120, 128), F32),
            pltpu.VMEM((2, 6, 120, 128), F32),
            pltpu.VMEM((1024, 128), F32),
            pltpu.VMEM((768, 128), F32),
            pltpu.VMEM(rows, F32),
            pltpu.VMEM(rows, F32),
            pltpu.VMEM(rows, F32),
            pltpu.VMEM(rows, F32),
            pltpu.VMEM((112, 256), F32),
            pltpu.VMEM((2, 17, 64, 512), BF16),
            pltpu.SemaphoreType.DMA((nb // GROUP,)),
            pltpu.SemaphoreType.DMA((3,)),
            pltpu.SemaphoreType.DMA((3, 3)),
            pltpu.SemaphoreType.DMA((2, 2)),
            pltpu.SemaphoreType.DMA((2, 2, 2)),
        ],
        compiler_params=pltpu.CompilerParams(
            collective_id=0, has_side_effects=True, vmem_limit_bytes=50 * 2**20
        ),
    )(source_block, sb, cutoff, id_rows, blocks, weights)
    return remapped.reshape(6, 64, 225), filtered.reshape(6, 64, 225)


def solution(mesh):
    in_specs = (
        P(None, ("band", "col")),
        P(("band", "col"), None, None),
        P(("band", "col")),
        P(("band", "col"), None),
        P(("band", "col")),
        P(("band", "col")),
    )
    out_specs = (P(None, "band", "col"), P(None, "band", "col"))
    return jax.shard_map(local, mesh=mesh, in_specs=in_specs, out_specs=out_specs, check_vma=False)
```

time: 93.4 us -> 79.9 us (0.86)
  the two profiles are of different devices: /device:TPU:16 before, /device:TPU:24 now
where the time goes in v3:
time: 79.9 us; the launch traced here: 80 us
  Pallas kernels  73.4 us (92%)
  local copies, waits for them, and re-layouts  4.06 us (5%)
  other arithmetic  1.86 us (2%)
    pallas_call x1, Pallas kernels, local(): pl.pallas_call(kernel, name='remap', out_shape=[jax.ShapeDtypeStruct((384...  73.4 us
    unnamed x8, local copies, waits for them, and re-layouts  3.77 us

profile of v3, /device:TPU:24, one launch (start us, length us, event | category | flops | bytes accessed | tf_op | source)
XLA Modules:
  0.0 80.0 jit_solution(1142726823693749837)
XLA Ops:
  0.6 0.9 %convert_reduce_fusion = s32[256]{0:T(256)S(1)} fusion(s32[256]{0:T(256)} %bitcast.9), kind=kLoop, calls=%fused_computation.2 | loop fusion | flops 327424 | bytes 2048 | tf_op jit(solution)/shard_map/reduce_sum | solution.py:454
  1.6 0.7 add_add_fusion
  2.3 0.2 select_reduce_fusion
  2.5 0.2 gt.8
  2.6 0.1 sub.30
  2.8 0.0 copy-start
  2.8 0.9 %copy-done = bf16[6,16384]{1,0:T(8,128)(2,1)S(1)} copy-done((bf16[6,16384]{1,0:T(8,128)(2,1)S(1)}, bf16[6,16384]{1,0:T(8,128)(2,1)}, u32[]{:S(2)}) %copy-start) | copy-done | bytes 196632
  3.8 0.0 copy-start.1
  3.8 0.7 copy-done.1
  4.5 0.0 copy-start.2
  4.5 0.7 copy-done.2
  5.1 73.4 %remap.1 = (f32[384,225]{1,0:T(8,128)S(1)}, f32[384,225]{1,0:T(8,128)S(1)}) custom-call(s32[256]{0:T(256)S(1)} %copy-done.1, s32[576]{0:T(1024)S(1)} %get-tuple-element.7.sb_ref, s32[2]{0:T(128)S(1)} %copy-done.2, f32[96,128]{1,0:T(8,128)S(1)} %pad.4.id_ref, bf16[128,6,128]{2,1,0:T(8,128)(2,1)S(1)} %bitcast.8, bf16[256,128,128]{2,1,0:T(8,128)(2,1)} %w_ref.1), custom_call_target="tpu_custom_call" | custom-call | tf_op jit(solution)/shard_map/remap/pallas_call | solution.py:466
  78.5 0.7 copy.10
  79.3 0.7 copy.11
  (4 shorter events, 0.1 us)
Async XLA Ops:
  2.8 1.0 %copy-start = (bf16[6,16384]{1,0:T(8,128)(2,1)S(1)}, bf16[6,16384]{1,0:T(8,128)(2,1)}, u32[]{:S(2)}) copy-start(bf16[6,16384]{1,0:T(8,128)(2,1)} %param.6) | copy-start | bytes 589828
  3.8 0.7 copy-start.1
  4.5 0.7 copy-start.2

commit v4 on v3

--- a/solution.py
+++ b/solution.py
@@ -168,10 +168,32 @@
         base[start + count : start + 2 * count, :] = jnp.where(i < 225, jnp.sin(angle), 0.0)
 
 
+def slot_table(meta_ref, band, cols, slot_ref, id_ref):
+    nt = (((1,), (1,)), ((), ()))
+    nb = meta_ref.shape[1]
+    owner = meta_ref[0:1, :] - (band - 1) * cols
+    sub = lax.broadcasted_iota(jnp.int32, (nb, nb), 0)
+    lane = lax.broadcasted_iota(jnp.int32, (nb, nb), 1)
+    across = jnp.broadcast_to(owner, (nb, nb))
+    down = jnp.transpose(across)
+    earlier = jnp.where((down == across) & (sub < lane), 1, 0)
+    rank = jnp.sum(earlier, axis=0, keepdims=True)
+    rank_down = jnp.transpose(jnp.broadcast_to(rank, (128, nb)))
+    near = down[:, 0:128] == lane[:, 0:128]
+    for s in range(CAP):
+        here = jnp.where(near & (rank_down == s), sub[:, 0:128], 0)
+        slot_ref[s : s + 1, :] = jnp.sum(here, axis=0, keepdims=True)
+    number = lax.broadcasted_iota(jnp.int32, (128, nb), 0)
+    to = (jnp.broadcast_to(owner, (128, nb)) == number).astype(F32).astype(BF16)
+    tile = (meta_ref[1:2, :] + 1).astype(F32)
+    tiles = jnp.where(jnp.broadcast_to(rank, (128, nb)) == number, tile, 0.0).astype(BF16)
+    id_ref[...] = lax.dot_general(to, tiles, nt, preferred_element_type=F32) - 1.0
+
+
 def kernel(
-    pick_ref, sb_ref, cut_ref, id_ref, src_ref, w_ref, remap_ref, filt_ref,
-    wbuf, part, send, recv, data, own, dtx, drx, tiles, flat, rtx, rrx, ztx, zrx, base, table,
-    w_sem, send_sem, recv_sem, dense_sem, row_sem,
+    meta_ref, src_ref, w_ref, remap_ref, filt_ref,
+    pick_ref, slot_ref, sb_ref, id_ref, wbuf, part, send, recv, data, own, dtx, drx, tiles, flat, rtx, rrx, ztx, zrx, base, table,
+    in_sem, w_sem, send_sem, recv_sem, dense_sem, row_sem, pair_sem,
 ):
     bands = lax.axis_size("band")
     band, col = lax.axis_index("band"), lax.axis_index("col")
@@ -179,6 +201,9 @@
     cols = NZ * NX
     planes = {0: (0, 1), 1: (1, 5), 2: (5, 8)}
 
+    pick_copy = pltpu.make_async_copy(meta_ref.at[2:4], pick_ref, in_sem.at[0])
+    pick_copy.start()
+
     def weight_copy(g):
         return pltpu.make_async_copy(
             w_ref.at[pl.ds(g * GROUP, GROUP)], wbuf.at[pl.ds(g * GROUP, GROUP)], w_sem.at[g]
@@ -214,6 +239,9 @@
                 first = d * 3 * NX + side * NX
                 recv[first : first + NX] = jnp.full((NX, *recv.shape[1:]), -1.0, F32)
 
+    pick_copy.wait()
+    table_copy = pltpu.make_async_copy(slot_ref, sb_ref, in_sem.at[1])
+
     for g in range(groups):
         weight_copy(g).wait()
 
@@ -221,10 +249,13 @@
             first = g * GROUP + i * 8
             for n in range(8):
                 k = first + n
-                part[k] = jnp.dot(src_ref[pick_ref[k]], wbuf[k], preferred_element_type=F32)
+                part[k] = jnp.dot(src_ref[pick_ref[0, k]], wbuf[k], preferred_element_type=F32)
             return carry
 
         lax.fori_loop(0, GROUP // 8, some, 0)
+        if g == 0:
+            slot_table(meta_ref, band, cols, slot_ref, id_ref)
+            table_copy.start()
 
     def turn(parity):
         return 1 - 2 * (parity & 1)
@@ -244,7 +275,7 @@
             c, _, _ = route(i, off)
             j = off * cols + c
             for s in range(CAP):
-                send[off, c, pl.ds(s, 6, stride=CAP), :] = part[sb_ref[j * CAP + s]]
+                send[off, c, pl.ds(s, 6, stride=CAP), :] = part[sb_ref[s, j]]
             send[off, c, 36:37, :] = id_ref[pl.ds(j, 1), :]
 
     def transmit(i):
@@ -264,6 +295,7 @@
                     device_id_type=MESH,
                 ).start()
 
+    table_copy.wait()
     pack(0)
     inner = (band > 0).astype(jnp.int32) + (band < bands - 1).astype(jnp.int32)
     pl.semaphore_wait(barrier, cols - 1 + cols * inner)
@@ -357,6 +389,9 @@
             own[0:120, 128 * lev : 128 * lev + 128] + drx[0, lev] + drx[1, lev]
         )
 
+    pl.semaphore_signal(pair_sem, inc=1, device_id=(band + turn(band), col), device_id_type=MESH)
+    pl.semaphore_wait(pair_sem, 1)
+
     def row(lat):
         t, s = divmod(225 * lat, 128)
         a, b, c = (tiles[8 * (t + n) : 8 * (t + n) + 8, :] for n in range(3))
@@ -417,7 +452,7 @@
             ztx[j, c, 0:6, :] = value[0:6, 0:128]
             ztx[j, c, 6:12, :] = value[0:6, 128:256]
 
-        zonal(get, put, table, cut_ref[j])
+        zonal(get, put, table, pick_ref[1, j])
         swap(ztx, zrx, 1, j)
 
     pltpu.make_async_copy(
@@ -445,31 +480,22 @@
 def local(source, weights, source_block, owner_device, target_tile, cutoff):
     cols = lax.axis_size("col")
     levels, nb, width = 6, weights.shape[0], weights.shape[1]
-    band = lax.axis_index("band")
     blocks = jnp.transpose(source.reshape(levels, -1, width), (1, 0, 2))
-    owners = owner_device[:, 0]
-    row = lax.broadcasted_iota(jnp.int32, (nb, nb), 0)
-    column = lax.broadcasted_iota(jnp.int32, (nb, nb), 1)
-    earlier = (owners[None, :] == owners[:, None]) & (column < row)
-    rank = jnp.sum(earlier.astype(jnp.int32), axis=1)
-    slot = (owners - (band - 1) * cols) * CAP + rank
-    total = 3 * cols * CAP
-    hit = lax.broadcasted_iota(jnp.int32, (total, nb), 0) == slot[None, :]
-    both = jnp.arange(nb, dtype=jnp.int32) * 128 + target_tile
-    code = jnp.sum(jnp.where(hit, both[None, :] + 1, 0), axis=1)
-    sb = jnp.maximum(code - 1, 0) // 128
-    tid = jnp.where(code > 0, (code - 1) % 128, -1).astype(F32)
-    id_rows = jnp.pad(tid.reshape(3 * cols, CAP), ((0, 0), (0, 128 - CAP)), constant_values=-1.0)
+    limit = jnp.pad(cutoff, (0, nb - cutoff.shape[0]))
+    meta = jnp.stack([owner_device[:, 0], target_tile, source_block, limit])
     vmem = pl.BlockSpec(memory_space=pltpu.VMEM)
-    smem = pl.BlockSpec(memory_space=pltpu.SMEM)
     rows = (2, cols, 16, 128)
     remapped, filtered = pl.pallas_call(
         kernel,
         name="remap",
         out_shape=[jax.ShapeDtypeStruct((384, 225), F32)] * 2,
-        in_specs=[smem, smem, smem, vmem, vmem, pl.BlockSpec(memory_space=pl.ANY)],
+        in_specs=[vmem, vmem, pl.BlockSpec(memory_space=pl.ANY)],
         out_specs=[vmem, vmem],
         scratch_shapes=[
+            pltpu.SMEM((2, nb), jnp.int32),
+            pltpu.VMEM((8, 128), jnp.int32),
+            pltpu.SMEM((8, 128), jnp.int32),
+            pltpu.VMEM((128, 128), F32),
             pltpu.VMEM((nb, width, width), BF16),
             pltpu.VMEM((nb, 6, 128), F32),
             pltpu.VMEM((3, cols, ROWS, 128), F32),
@@ -486,16 +512,18 @@
             pltpu.VMEM(rows, F32),
             pltpu.VMEM((112, 256), F32),
             pltpu.VMEM((2, 17, 64, 512), BF16),
+            pltpu.SemaphoreType.DMA((2,)),
             pltpu.SemaphoreType.DMA((nb // GROUP,)),
             pltpu.SemaphoreType.DMA((3,)),
             pltpu.SemaphoreType.DMA((3, 3)),
             pltpu.SemaphoreType.DMA((2, 2)),
             pltpu.SemaphoreType.DMA((2, 2, 2)),
+            pltpu.SemaphoreType.REGULAR,
         ],
         compiler_params=pltpu.CompilerParams(
             collective_id=0, has_side_effects=True, vmem_limit_bytes=50 * 2**20
         ),
-    )(source_block, sb, cutoff, id_rows, blocks, weights)
+    )(meta, blocks, weights)
     return remapped.reshape(6, 64, 225), filtered.reshape(6, 64, 225)
 
 

time: 79.9 us -> 74 us (0.926)
  the two profiles are of different devices: /device:TPU:24 before, /device:TPU:16 now
where the time goes in v4:
time: 74 us; the launch traced here: 73.3 us
  Pallas kernels  68.8 us (93%)
  local copies, waits for them, and re-layouts  3.1 us (4%)
    pallas_call x1, Pallas kernels, local(): pl.pallas_call(kernel, name='remap', out_shape=[jax.ShapeDtypeStruct((384...  68.8 us
    unnamed x4, local copies, waits for them, and re-layouts  2.44 us

profile of v4, /device:TPU:16, one launch (start us, length us, event | category | flops | bytes accessed | tf_op | source)
XLA Modules:
  0.0 73.3 jit_solution(158774320176537934)
XLA Ops:
  0.6 0.7 pad.4
  1.3 0.7 pad_add_fusion.meta_ref
  2.0 0.0 copy-start
  2.0 0.9 %copy-done = bf16[6,16384]{1,0:T(8,128)(2,1)S(1)} copy-done((bf16[6,16384]{1,0:T(8,128)(2,1)S(1)}, bf16[6,16384]{1,0:T(8,128)(2,1)}, u32[]{:S(2)}) %copy-start) | copy-done | bytes 196632
  3.0 68.8 %remap.1 = (f32[384,225]{1,0:T(8,128)S(1)}, f32[384,225]{1,0:T(8,128)S(1)}) custom-call(s32[4,256]{1,0:T(4,128)S(1)} %pad_add_fusion.meta_ref, bf16[128,6,128]{2,1,0:T(8,128)(2,1)S(1)} %bitcast.11, bf16[256,128,128]{2,1,0:T(8,128)(2,1)} %w_ref.1), custom_call_target="tpu_custom_call" | custom-call | tf_op jit(solution)/shard_map/remap/pallas_call | solution.py:488
  71.8 0.7 %copy.10 = f32[6,64,225]{2,1,0:T(8,128)} copy(f32[6,64,225]{2,1,0:T(8,128)S(1)} %bitcast.10) | data formatting | bytes 691200
  72.5 0.7 %copy.11 = f32[6,64,225]{2,1,0:T(8,128)} copy(f32[6,64,225]{2,1,0:T(8,128)S(1)} %bitcast.9) | data formatting | bytes 691200
Async XLA Ops:
  2.0 1.0 %copy-start = (bf16[6,16384]{1,0:T(8,128)(2,1)S(1)}, bf16[6,16384]{1,0:T(8,128)(2,1)}, u32[]{:S(2)}) copy-start(bf16[6,16384]{1,0:T(8,128)(2,1)} %param.6) | copy-start | bytes 589828

commit v5 on v4

--- a/solution.py
+++ b/solution.py
@@ -118,7 +118,8 @@
                 table[1, r, row : row + 16, 256 * half : 256 * half + 256] = lo
 
 
-def scale_at(r, limit):
+def scale_at(r, limits):
+    limit = jnp.where(lax.broadcasted_iota(jnp.int32, (8, 64), 0) < 3, limits[0], limits[1])
     n = lax.broadcasted_iota(jnp.int32, (8, 64), 1)
     mirror = n >= 32
     k = 32 * (n & 15) + jnp.where(mirror, 32 - r, r)
@@ -131,7 +132,7 @@
     return jnp.where(keep, weight, 0.0).astype(F32)
 
 
-def zonal(get, put, table, limit):
+def zonal(get, put, table, limits):
     spec = real_dft([get(c) for c in range(32)])
     nt = (((1,), (1,)), ((), ()))
     nn = (((1,), (0,)), ((), ()))
@@ -147,7 +148,7 @@
     for r in range(17):
         re, im = spec[r]
         im = jnp.zeros_like(re) if im is None else im
-        s = product(jnp.concatenate([re, im], axis=1), r, nt) * scale_at(r, limit)
+        s = product(jnp.concatenate([re, im], axis=1), r, nt) * scale_at(r, limits)
         w = product(s, r, nn)
         back.append((w[:, 0:256], None if r in (0, 16) else w[:, 256:512]))
     for c, value in enumerate(real_idft(back, 32)):
@@ -170,8 +171,8 @@
 
 def slot_table(meta_ref, band, cols, slot_ref, id_ref):
     nt = (((1,), (1,)), ((), ()))
-    nb = meta_ref.shape[1]
-    owner = meta_ref[0:1, :] - (band - 1) * cols
+    nb = 2 * meta_ref.shape[1]
+    owner = jnp.concatenate([meta_ref[0:1, :], meta_ref[1:2, :]], axis=1) - (band - 1) * cols
     sub = lax.broadcasted_iota(jnp.int32, (nb, nb), 0)
     lane = lax.broadcasted_iota(jnp.int32, (nb, nb), 1)
     across = jnp.broadcast_to(owner, (nb, nb))
@@ -185,13 +186,13 @@
         slot_ref[s : s + 1, :] = jnp.sum(here, axis=0, keepdims=True)
     number = lax.broadcasted_iota(jnp.int32, (128, nb), 0)
     to = (jnp.broadcast_to(owner, (128, nb)) == number).astype(F32).astype(BF16)
-    tile = (meta_ref[1:2, :] + 1).astype(F32)
+    tile = (jnp.concatenate([meta_ref[2:3, :], meta_ref[3:4, :]], axis=1) + 1).astype(F32)
     tiles = jnp.where(jnp.broadcast_to(rank, (128, nb)) == number, tile, 0.0).astype(BF16)
     id_ref[...] = lax.dot_general(to, tiles, nt, preferred_element_type=F32) - 1.0
 
 
 def kernel(
-    meta_ref, src_ref, w_ref, remap_ref, filt_ref,
+    meta_ref, src_ref, w_ref, out_ref,
     pick_ref, slot_ref, sb_ref, id_ref, wbuf, part, send, recv, data, own, dtx, drx, tiles, flat, rtx, rrx, ztx, zrx, base, table,
     in_sem, w_sem, send_sem, recv_sem, dense_sem, row_sem, pair_sem,
 ):
@@ -201,7 +202,7 @@
     cols = NZ * NX
     planes = {0: (0, 1), 1: (1, 5), 2: (5, 8)}
 
-    pick_copy = pltpu.make_async_copy(meta_ref.at[2:4], pick_ref, in_sem.at[0])
+    pick_copy = pltpu.make_async_copy(meta_ref, pick_ref, in_sem.at[0])
     pick_copy.start()
 
     def weight_copy(g):
@@ -247,9 +248,10 @@
 
         def some(i, carry, g=g):
             first = g * GROUP + i * 8
+            lane = g * GROUP % 128 + i * 8
             for n in range(8):
                 k = first + n
-                part[k] = jnp.dot(src_ref[pick_ref[0, k]], wbuf[k], preferred_element_type=F32)
+                part[k] = jnp.dot(src_ref[pick_ref[4 + g * GROUP // 128, lane + n]], wbuf[k], preferred_element_type=F32)
             return carry
 
         lax.fori_loop(0, GROUP // 8, some, 0)
@@ -262,7 +264,7 @@
 
     def route(i, off):
         u = i // NX
-        delta = jnp.where(u < 3, 5 + u, 7 - u)
+        delta = jnp.where(u < 4, 4 - u, lax.rem(u + 1, NZ))
         s = turn(band + off - 1)
         owner_z = lax.rem(z - s * delta + 2 * NZ, NZ)
         shift = jnp.where(delta == 0, 0, jnp.where(delta <= 4, s, -s))
@@ -335,7 +337,7 @@
                 def _(wait=wait):
                     wait.wait()
 
-    def summed(group):
+    def summed(group, put):
         first, last = (3 * NX * p for p in planes[group])
         n = last - first
 
@@ -356,41 +358,37 @@
         spread = jnp.dot(diag, jnp.ones((128, 128), BF16), preferred_element_type=F32)
         tile = lax.broadcasted_iota(jnp.int32, (8 * n, 128), 1).astype(F32)
         chooser = (spread == tile).astype(F32).astype(BF16)
-        hi, lo = halves(data[8 * first : 8 * last, :])
         tn = (((0,), (0,)), ((), ()))
-        return lax.dot_general(chooser, hi, tn, preferred_element_type=F32) + lax.dot_general(
-            chooser, lo, tn, preferred_element_type=F32
-        )
-
-    def dense(which, to):
+        for h in range(2):
+            hi, lo = halves(data[8 * first : 8 * last, 384 * h : 384 * h + 384])
+            put(
+                h,
+                lax.dot_general(chooser, hi, tn, preferred_element_type=F32)
+                + lax.dot_general(chooser, lo, tn, preferred_element_type=F32),
+            )
+
+    def dense(which, h, to):
         return pltpu.make_async_remote_copy(
-            src_ref=dtx.at[which, :, 0:113],
-            dst_ref=drx.at[which, :, 0:113],
-            send_sem=dense_sem.at[which, 0],
-            recv_sem=dense_sem.at[which, 1],
+            src_ref=dtx.at[which, 3 * h : 3 * h + 3, 0:113],
+            dst_ref=drx.at[which, 3 * h : 3 * h + 3, 0:113],
+            send_sem=dense_sem.at[which, h, 0],
+            recv_sem=dense_sem.at[which, h, 1],
             device_id=(band, to),
             device_id_type=MESH,
         )
 
-    for group, which, to in ((2, 1, up), (0, None, None), (1, 0, down)):
+    def keep_own(h, total):
+        own[:, 384 * h : 384 * h + 384] = total
+
+    for group, which, to in ((1, 0, down), (0, None, None), (2, 1, up)):
         take(group)
-        total = summed(group)
-        if which is None:
-            own[...] = total
-            continue
-        for lev in range(6):
-            dtx[which, lev] = total[0:120, 128 * lev : 128 * lev + 128]
-        dense(which, to).start()
-
-    dense(1, up).wait()
-    dense(0, down).wait()
-    for lev in range(6):
-        tiles[pl.ds(lev, 120, stride=8), :] = (
-            own[0:120, 128 * lev : 128 * lev + 128] + drx[0, lev] + drx[1, lev]
-        )
-
-    pl.semaphore_signal(pair_sem, inc=1, device_id=(band + turn(band), col), device_id_type=MESH)
-    pl.semaphore_wait(pair_sem, 1)
+
+        def pass_on(h, total, which=which, to=to):
+            for lev in range(3):
+                dtx[which, 3 * h + lev] = total[0:120, 128 * lev : 128 * lev + 128]
+            dense(which, h, to).start()
+
+        summed(group, keep_own if which is None else pass_on)
 
     def row(lat):
         t, s = divmod(225 * lat, 128)
@@ -399,7 +397,7 @@
             a, b, c = (pltpu.roll(v, 128 - s, 1) for v in (a, b, c))
             keep = lax.broadcasted_iota(jnp.int32, (8, 128), 1) < 128 - s
             a, b = jnp.where(keep, a, b), jnp.where(keep, b, c)
-        return a[0:6], b[0:6]
+        return a, b
 
     def swap(src, dst, which, j):
         def step(i, carry):
@@ -431,16 +429,29 @@
         part_of = src.at[j, 0 : cols - 1, 0:12]
         pltpu.make_async_copy(part_of, part_of, row_sem.at[which, j, 0]).wait()
 
-    for j in range(2):
-        for lat in range(j, 2 * cols, 2):
-            a, b = row(lat)
-            flat[pl.ds(lat, 6, stride=64), :] = a
-            flat[pl.ds(384 + lat, 6, stride=64), :] = b
-            rtx[j, lat // 2, 0:6, :] = a
-            rtx[j, lat // 2, 6:12, :] = b
-        swap(rtx, rrx, 0, j)
-    remap_ref[:, 0:128] = flat[0:384, :]
-    remap_ref[:, 128:225] = flat[384:768, 0:97]
+    for h in range(2):
+        dense(1, h, up).wait()
+        dense(0, h, down).wait()
+        for lev in range(3 * h, 3 * h + 3):
+            tiles[pl.ds(lev, 120, stride=8), :] = (
+                own[0:120, 128 * lev : 128 * lev + 128] + drx[0, lev] + drx[1, lev]
+            )
+        if h == 0:
+            pl.semaphore_signal(
+                pair_sem, inc=1, device_id=(band + turn(band), col), device_id_type=MESH
+            )
+        for lat in range(2 * cols):
+            a, b = (v[3 * h : 3 * h + 3] for v in row(lat))
+            flat[pl.ds(192 * h + lat, 3, stride=64), :] = a
+            flat[pl.ds(384 + 192 * h + lat, 3, stride=64), :] = b
+            first = 3 * (lat % 2)
+            rtx[h, lat // 2, first : first + 3, :] = a
+            rtx[h, lat // 2, 6 + first : 9 + first, :] = b
+        if h == 0:
+            pl.semaphore_wait(pair_sem, 1)
+        swap(rtx, rrx, 0, h)
+    out_ref[0, :, 0:128] = flat[0:384, :]
+    out_ref[0, :, 128:225] = flat[384:768, 0:97]
 
     for j in range(2):
         swapped(rrx, 0, j)
@@ -452,7 +463,7 @@
             ztx[j, c, 0:6, :] = value[0:6, 0:128]
             ztx[j, c, 6:12, :] = value[0:6, 128:256]
 
-        zonal(get, put, table, pick_ref[1, j])
+        zonal(get, put, table, (pick_ref[6, 0], pick_ref[6, 1]))
         swap(ztx, zrx, 1, j)
 
     pltpu.make_async_copy(
@@ -468,11 +479,12 @@
         swap_sent(rtx, 0, j)
     for j in range(2):
         swapped(zrx, 1, j)
-        for lat in range(j, 2 * cols, 2):
-            flat[pl.ds(lat, 6, stride=64), :] = zrx[j, lat // 2, 0:6, :]
-            flat[pl.ds(384 + lat, 6, stride=64), :] = zrx[j, lat // 2, 6:12, :]
-    filt_ref[:, 0:128] = flat[0:384, :]
-    filt_ref[:, 128:225] = flat[384:768, 0:97]
+        for lat in range(2 * cols):
+            first = 3 * (lat % 2)
+            flat[pl.ds(192 * j + lat, 3, stride=64), :] = zrx[j, lat // 2, first : first + 3, :]
+            flat[pl.ds(384 + 192 * j + lat, 3, stride=64), :] = zrx[j, lat // 2, 6 + first : 9 + first, :]
+    out_ref[1, :, 0:128] = flat[0:384, :]
+    out_ref[1, :, 128:225] = flat[384:768, 0:97]
     for j in range(2):
         swap_sent(ztx, 1, j)
 
@@ -481,18 +493,18 @@
     cols = lax.axis_size("col")
     levels, nb, width = 6, weights.shape[0], weights.shape[1]
     blocks = jnp.transpose(source.reshape(levels, -1, width), (1, 0, 2))
-    limit = jnp.pad(cutoff, (0, nb - cutoff.shape[0]))
-    meta = jnp.stack([owner_device[:, 0], target_tile, source_block, limit])
+    spare = jnp.zeros((nb - cutoff.shape[0],), jnp.int32)
+    meta = jnp.concatenate([owner_device[:, 0], target_tile, source_block, cutoff, spare]).reshape(8, nb // 2)
     vmem = pl.BlockSpec(memory_space=pltpu.VMEM)
     rows = (2, cols, 16, 128)
-    remapped, filtered = pl.pallas_call(
+    both = pl.pallas_call(
         kernel,
         name="remap",
-        out_shape=[jax.ShapeDtypeStruct((384, 225), F32)] * 2,
+        out_shape=jax.ShapeDtypeStruct((2, 384, 225), F32),
         in_specs=[vmem, vmem, pl.BlockSpec(memory_space=pl.ANY)],
-        out_specs=[vmem, vmem],
+        out_specs=vmem,
         scratch_shapes=[
-            pltpu.SMEM((2, nb), jnp.int32),
+            pltpu.SMEM((8, nb // 2), jnp.int32),
             pltpu.VMEM((8, 128), jnp.int32),
             pltpu.SMEM((8, 128), jnp.int32),
             pltpu.VMEM((128, 128), F32),
@@ -516,7 +528,7 @@
             pltpu.SemaphoreType.DMA((nb // GROUP,)),
             pltpu.SemaphoreType.DMA((3,)),
             pltpu.SemaphoreType.DMA((3, 3)),
-            pltpu.SemaphoreType.DMA((2, 2)),
+            pltpu.SemaphoreType.DMA((2, 2, 2)),
             pltpu.SemaphoreType.DMA((2, 2, 2)),
             pltpu.SemaphoreType.REGULAR,
         ],
@@ -524,7 +536,7 @@
             collective_id=0, has_side_effects=True, vmem_limit_bytes=50 * 2**20
         ),
     )(meta, blocks, weights)
-    return remapped.reshape(6, 64, 225), filtered.reshape(6, 64, 225)
+    return both[0].reshape(6, 64, 225), both[1].reshape(6, 64, 225)
 
 
 def solution(mesh):

time: 74 us -> 71 us (0.959)
  Pallas kernels: 68.8 us -> 67.4 us
    unnamed x4 -> x2, local copies, waits for them, and re-layouts: 2.44 us -> 0.95 us
    pallas_call x1, Pallas kernels: 68.8 us -> 67.4 us  [local(): pl.pallas_call(kernel, name='remap', out_shape=jax.ShapeDtypeStruct((2, 3...]
    slice x0 -> x1, local copies, waits for them, and re-layouts: none -> 0.93 us  [local(): return (both[0].reshape(6, 64, 225), both[1].reshape(6, 64, 225))]
    concatenate x0 -> x1, local copies, waits for them, and re-layouts: none -> 0.79 us  [local(): jnp.concatenate([owner_device[:, 0], target_tile, source_block, cutoff, s...]
where the time goes in v5:
time: 71 us; the launch traced here: 70.7 us
  Pallas kernels  67.4 us (95%)
  local copies, waits for them, and re-layouts  2.67 us (4%)
    pallas_call x1, Pallas kernels, local(): pl.pallas_call(kernel, name='remap', out_shape=jax.ShapeDtypeStruct((2, 3...  67.4 us

profile of v5, /device:TPU:16, one launch (start us, length us, event | category | flops | bytes accessed | tf_op | source)
XLA Modules:
  0.0 70.7 jit_solution(7326892101246091492)
XLA Ops:
  0.6 0.8 %concatenate.3 = s32[1024]{0:T(1024)S(1)} concatenate(s32[256]{0:T(256)} %bitcast.11, s32[256]{0:T(256)} %param.10, s32[256]{0:T(256)} %param.8, s32[2]{0:T(128)} %param.11, s32[254]{0:T(256)S(1)} %broadcast_in_dim.3), dimensions={0} | concatenate | bytes 8192 | tf_op jit(solution)/shard_map/concatenate | solution.py:497
  1.4 0.0 copy-start
  1.4 0.9 %copy-done = bf16[6,16384]{1,0:T(8,128)(2,1)S(1)} copy-done((bf16[6,16384]{1,0:T(8,128)(2,1)S(1)}, bf16[6,16384]{1,0:T(8,128)(2,1)}, u32[]{:S(2)}) %copy-start) | copy-done | bytes 196632
  2.4 67.4 %remap.1 = f32[2,384,225]{2,1,0:T(8,128)S(1)} custom-call(s32[8,128]{1,0:T(8,128)S(1)} %bitcast.8, bf16[128,6,128]{2,1,0:T(8,128)(2,1)S(1)} %bitcast.7, bf16[256,128,128]{2,1,0:T(8,128)(2,1)} %w_ref.1), custom_call_target="tpu_custom_call" | custom-call | tf_op jit(solution)/shard_map/remap/pallas_call | solution.py:500
  69.8 0.9 %fusion = (f32[1,384,225]{2,1,0:T(8,128)}, f32[1,384,225]{2,1,0:T(8,128)}) fusion(f32[2,384,225]{2,1,0:T(8,128)S(1)} %remap.1), kind=kLoop, calls=%fused_computation | loop fusion | bytes 1382400 | tf_op jit(solution)/shard_map/slice | solution.py:539
  (1 shorter events, 0.0 us)
Async XLA Ops:
  1.4 0.9 %copy-start = (bf16[6,16384]{1,0:T(8,128)(2,1)S(1)}, bf16[6,16384]{1,0:T(8,128)(2,1)}, u32[]{:S(2)}) copy-start(bf16[6,16384]{1,0:T(8,128)(2,1)} %param.6) | copy-start | bytes 589828

commit v6 on v5

--- a/solution.py
+++ b/solution.py
@@ -200,7 +200,7 @@
     band, col = lax.axis_index("band"), lax.axis_index("col")
     z, x = col // NX, lax.rem(col, NX)
     cols = NZ * NX
-    planes = {0: (0, 1), 1: (1, 5), 2: (5, 8)}
+    planes = {0: (0, 1), 1: (2, 5), 2: (5, 8), 3: (1, 2)}
 
     pick_copy = pltpu.make_async_copy(meta_ref, pick_ref, in_sem.at[0])
     pick_copy.start()
@@ -264,10 +264,10 @@
 
     def route(i, off):
         u = i // NX
-        delta = jnp.where(u < 4, 4 - u, lax.rem(u + 1, NZ))
+        delta = jnp.where(u < 3, 4 - u, jnp.where(u == 3, 5, jnp.where(u == 4, 1, lax.rem(u + 1, NZ))))
         s = turn(band + off - 1)
         owner_z = lax.rem(z - s * delta + 2 * NZ, NZ)
-        shift = jnp.where(delta == 0, 0, jnp.where(delta <= 4, s, -s))
+        shift = jnp.where(delta <= 1, delta * s, jnp.where(delta <= 4, 2 * s, -s))
         plane = lax.rem(owner_z + shift + NZ, NZ)
         to_x = lax.rem(x + i, NX)
         return owner_z * NX + to_x, delta, plane * NX + to_x
@@ -284,7 +284,7 @@
         for off in (0, 2, 1):
             c, delta, to = route(i, off)
             ok = to != col if off == 1 else valid(off)
-            group = jnp.where(delta == 0, 0, jnp.where(delta <= 4, 1, 2))
+            group = jnp.where(delta <= 1, 3 * delta, jnp.where(delta <= 4, 1, 2))
 
             @pl.when(ok)
             def _(off=off, c=c, delta=delta, to=to, group=group):
@@ -314,7 +314,8 @@
     mine = turn(band)
     up = lax.rem(z + mine + NZ, NZ) * NX + x
     down = lax.rem(z - mine + NZ, NZ) * NX + x
-    for c, delta, group in ((col, 0, 0), (down, 1, 1), (up, 7, 2)):
+    down2 = lax.rem(z - 2 * mine + NZ, NZ) * NX + x
+    for c, delta, group in ((col, 0, 0), (down, 1, 3), (down2, 2, 1), (up, 7, 2)):
         pltpu.make_async_copy(
             send.at[1, c, 0:SENT],
             recv.at[delta * 3 * NX + NX + x, 0:SENT],
@@ -377,18 +378,30 @@
             device_id_type=MESH,
         )
 
-    def keep_own(h, total):
+    def keep(h, total):
         own[:, 384 * h : 384 * h + 384] = total
 
-    for group, which, to in ((1, 0, down), (0, None, None), (2, 1, up)):
-        take(group)
-
-        def pass_on(h, total, which=which, to=to):
+    def pass_on(which, to):
+        def put(h, total):
             for lev in range(3):
                 dtx[which, 3 * h + lev] = total[0:120, 128 * lev : 128 * lev + 128]
             dense(which, h, to).start()
 
-        summed(group, keep_own if which is None else pass_on)
+        return put
+
+    take(1)
+    summed(1, pass_on(2, down))
+    take(3)
+    summed(3, keep)
+    for h in range(2):
+        dense(2, h, down).wait()
+        for lev in range(3 * h, 3 * h + 3):
+            dtx[0, lev] = own[0:120, 128 * lev : 128 * lev + 128] + drx[2, lev]
+        dense(0, h, down).start()
+    take(2)
+    summed(2, pass_on(1, up))
+    take(0)
+    summed(0, keep)
 
     def row(lat):
         t, s = divmod(225 * lat, 128)
@@ -467,7 +480,7 @@
         swap(ztx, zrx, 1, j)
 
     pltpu.make_async_copy(
-        send.at[1, 0 : cols - 3, 0:SENT], send.at[1, 0 : cols - 3, 0:SENT], send_sem.at[1]
+        send.at[1, 0 : cols - 4, 0:SENT], send.at[1, 0 : cols - 4, 0:SENT], send_sem.at[1]
     ).wait()
     for off in (0, 2):
 
@@ -514,8 +527,8 @@
             pltpu.VMEM((3 * cols, ROWS, 128), F32),
             pltpu.VMEM((24 * cols, 768), F32),
             pltpu.VMEM((128, 768), F32),
-            pltpu.VMEM((2, 6, 120, 128), F32),
-            pltpu.VMEM((2, 6, 120, 128), F32),
+            pltpu.VMEM((3, 6, 120, 128), F32),
+            pltpu.VMEM((3, 6, 120, 128), F32),
             pltpu.VMEM((1024, 128), F32),
             pltpu.VMEM((768, 128), F32),
             pltpu.VMEM(rows, F32),
@@ -527,8 +540,8 @@
             pltpu.SemaphoreType.DMA((2,)),
             pltpu.SemaphoreType.DMA((nb // GROUP,)),
             pltpu.SemaphoreType.DMA((3,)),
-            pltpu.SemaphoreType.DMA((3, 3)),
-            pltpu.SemaphoreType.DMA((2, 2, 2)),
+            pltpu.SemaphoreType.DMA((4, 3)),
+            pltpu.SemaphoreType.DMA((3, 2, 2)),
             pltpu.SemaphoreType.DMA((2, 2, 2)),
             pltpu.SemaphoreType.REGULAR,
         ],

time: 71 us -> 69 us (0.972)
  Pallas kernels: 67.4 us -> 65.6 us
    pallas_call x1, Pallas kernels: 67.4 us -> 65.6 us  [local(): pl.pallas_call(kernel, name='remap', out_shape=jax.ShapeDtypeStruct((2, 3...]
where the time goes in v6:
time: 69 us; the launch traced here: 68.9 us
  Pallas kernels  65.6 us (95%)
  local copies, waits for them, and re-layouts  2.67 us (4%)
    pallas_call x1, Pallas kernels, local(): pl.pallas_call(kernel, name='remap', out_shape=jax.ShapeDtypeStruct((2, 3...  65.6 us

profile of v6, /device:TPU:16, one launch (start us, length us, event | category | flops | bytes accessed | tf_op | source)
XLA Modules:
  0.0 68.9 jit_solution(565086045342592602)
XLA Ops:
  0.6 0.8 %concatenate.3 = s32[1024]{0:T(1024)S(1)} concatenate(s32[256]{0:T(256)} %bitcast.11, s32[256]{0:T(256)} %param.10, s32[256]{0:T(256)} %param.8, s32[2]{0:T(128)} %param.11, s32[254]{0:T(256)S(1)} %broadcast_in_dim.3), dimensions={0} | concatenate | bytes 8192 | tf_op jit(solution)/shard_map/concatenate | solution.py:510
  1.4 0.0 copy-start
  1.4 0.9 %copy-done = bf16[6,16384]{1,0:T(8,128)(2,1)S(1)} copy-done((bf16[6,16384]{1,0:T(8,128)(2,1)S(1)}, bf16[6,16384]{1,0:T(8,128)(2,1)}, u32[]{:S(2)}) %copy-start) | copy-done | bytes 196632
  2.4 65.6 %remap.1 = f32[2,384,225]{2,1,0:T(8,128)S(1)} custom-call(s32[8,128]{1,0:T(8,128)S(1)} %bitcast.8, bf16[128,6,128]{2,1,0:T(8,128)(2,1)S(1)} %bitcast.7, bf16[256,128,128]{2,1,0:T(8,128)(2,1)} %w_ref.1), custom_call_target="tpu_custom_call" | custom-call | tf_op jit(solution)/shard_map/remap/pallas_call | solution.py:513
  68.0 0.9 %fusion = (f32[1,384,225]{2,1,0:T(8,128)}, f32[1,384,225]{2,1,0:T(8,128)}) fusion(f32[2,384,225]{2,1,0:T(8,128)S(1)} %remap.1), kind=kLoop, calls=%fused_computation | loop fusion | bytes 1382400 | tf_op jit(solution)/shard_map/slice | solution.py:552
  (1 shorter events, 0.0 us)
Async XLA Ops:
  1.4 0.9 %copy-start = (bf16[6,16384]{1,0:T(8,128)(2,1)S(1)}, bf16[6,16384]{1,0:T(8,128)(2,1)}, u32[]{:S(2)}) copy-start(bf16[6,16384]{1,0:T(8,128)(2,1)} %param.6) | copy-start | bytes 589828

commit v7 on v6

--- a/solution.py
+++ b/solution.py
@@ -269,7 +269,7 @@
         owner_z = lax.rem(z - s * delta + 2 * NZ, NZ)
         shift = jnp.where(delta <= 1, delta * s, jnp.where(delta <= 4, 2 * s, -s))
         plane = lax.rem(owner_z + shift + NZ, NZ)
-        to_x = lax.rem(x + i, NX)
+        to_x = lax.rem(x + turn(band) * i + cols, NX)
         return owner_z * NX + to_x, delta, plane * NX + to_x
 
     def pack(i):
@@ -417,7 +417,7 @@
             u = i // NX
             m = (u + 1) // 2
             dz = jnp.where(lax.rem(u, 2) == 0, 4 + m, 4 - m)
-            to = lax.rem(z + dz, NZ) * NX + lax.rem(x + i, NX)
+            to = lax.rem(z + dz, NZ) * NX + lax.rem(x + turn(band) * i + cols, NX)
 
             @pl.when(to != col)
             def _():

time: 69 us -> 68.8 us (level)
  the two profiles are of different devices: /device:TPU:16 before, /device:TPU:1 now
where the time goes in v7:
time: 68.8 us; the launch traced here: 69 us
  Pallas kernels  65.7 us (95%)
  local copies, waits for them, and re-layouts  2.67 us (4%)
    pallas_call x1, Pallas kernels, local(): pl.pallas_call(kernel, name='remap', out_shape=jax.ShapeDtypeStruct((2, 3...  65.7 us

profile of v7, /device:TPU:1, one launch (start us, length us, event | category | flops | bytes accessed | tf_op | source)
XLA Modules:
  0.0 69.0 jit_solution(6484423806074863349)
XLA Ops:
  0.6 0.8 %concatenate.3 = s32[1024]{0:T(1024)S(1)} concatenate(s32[256]{0:T(256)} %bitcast.11, s32[256]{0:T(256)} %param.10, s32[256]{0:T(256)} %param.8, s32[2]{0:T(128)} %param.11, s32[254]{0:T(256)S(1)} %broadcast_in_dim.3), dimensions={0} | concatenate | bytes 8192 | tf_op jit(solution)/shard_map/concatenate | solution.py:510
  1.4 0.0 copy-start
  1.4 0.9 %copy-done = bf16[6,16384]{1,0:T(8,128)(2,1)S(1)} copy-done((bf16[6,16384]{1,0:T(8,128)(2,1)S(1)}, bf16[6,16384]{1,0:T(8,128)(2,1)}, u32[]{:S(2)}) %copy-start) | copy-done | bytes 196632
  2.4 65.7 %remap.1 = f32[2,384,225]{2,1,0:T(8,128)S(1)} custom-call(s32[8,128]{1,0:T(8,128)S(1)} %bitcast.8, bf16[128,6,128]{2,1,0:T(8,128)(2,1)S(1)} %bitcast.7, bf16[256,128,128]{2,1,0:T(8,128)(2,1)} %w_ref.1), custom_call_target="tpu_custom_call" | custom-call | tf_op jit(solution)/shard_map/remap/pallas_call | solution.py:513
  68.1 0.9 %fusion = (f32[1,384,225]{2,1,0:T(8,128)}, f32[1,384,225]{2,1,0:T(8,128)}) fusion(f32[2,384,225]{2,1,0:T(8,128)S(1)} %remap.1), kind=kLoop, calls=%fused_computation | loop fusion | bytes 1382400 | tf_op jit(solution)/shard_map/slice | solution.py:552
  (1 shorter events, 0.0 us)
Async XLA Ops:
  1.4 0.9 %copy-start = (bf16[6,16384]{1,0:T(8,128)(2,1)S(1)}, bf16[6,16384]{1,0:T(8,128)(2,1)}, u32[]{:S(2)}) copy-start(bf16[6,16384]{1,0:T(8,128)(2,1)} %param.6) | copy-start | bytes 589828
